TPU v7x, 32 devices: a whole 2x2x4 slice. The times are simulated.
32 devices in a mesh: sub: 16 (over z, y, core), col: 2 (over x).
Axes of the slice: x: 2, y: 2, z: 4, core: 2. Of those that a mesh axis runs over, the one named last changes fastest.
Arguments:
- interior_inverse: bfloat16 [16, 3072, 3072], P('sub', 'col'), may hold values from -1 to 2
- interface_coupling: bfloat16 [16, 3072, 512], P('sub', 'col'), may hold values from -0.109375 to 0.109375
- boundary_stiffness: float32 [16, 512, 512], P('sub', 'col'), may hold values from -3 to 3
- interior_mass: float32 [16, 3072], P('sub', 'col'), may hold values from 0.2 to 2
- boundary_mass: float32 [16, 512], P('sub', 'col'), may hold values from 0.2 to 2
- interior_modes: bfloat16 [16, 200, 3072], P('sub', None, 'col'), may hold values from -0.3125 to 0.3125
- block_map: int32 [16, 4], P('sub'), may hold values from 0 to 31, as said below
- trial_vectors: bfloat16 [64, 2, 2048], P(None, None, 'sub'), may hold values from -6 to 6
Outputs:
- reduced_stiffness: bfloat16 [2, 2048, 16, 256], P(None, 'sub', None, 'col')
- reduced_mass: bfloat16 [2, 2048, 16, 256], P(None, 'sub', None, 'col')
- modal_coupling: float32 [16, 64, 200], P('sub')
Inputs may be any that keep to these rules, and one draw needn't show every extreme that they name: `block_map`: row s lists the four blocks (s - 1) mod 16, s, ((s - 1) mod 16) + 16 and s + 16 in some order.
All inputs are finite; a program needn't handle non-finite values.
Results may differ from a plain program's by a relative error of at most 0.008.
Values may be sent and summed in bfloat16 or wider, within the bound.
No kernel may reach another device: no remote copies, remote signals or barrier semaphores. Data moves between devices by JAX's collectives and lax.ppermute only.
A program may use at most 64 MiB of HBM per device.

v0:
```python
import jax
import jax.numpy as jnp
from jax import lax
from jax.sharding import PartitionSpec as P


def shifted(block, axis, distance):
    devices = range(lax.axis_size(axis))
    route = [((i - distance) % len(devices), i) for i in devices]
    return lax.ppermute(block, axis, route)


def shards(
    interior_inverse,
    interface_coupling,
    boundary_stiffness,
    interior_mass,
    boundary_mass,
    interior_modes,
    block_map,
    trial_vectors,
):
    inverse_rows = interior_inverse[0]
    coupling_rows = interface_coupling[0]
    boundary_width = coupling_rows.shape[1]
    block_size = trial_vectors.shape[2]
    block_count = boundary_width // block_size
    sub_count = lax.axis_size("sub")
    grid_columns = lax.axis_size("col")
    sub_index = lax.axis_index("sub")
    column_index = lax.axis_index("col")
    previous_sub = (sub_index + sub_count - 1) % sub_count
    cycles = 2 * sub_count // grid_columns
    highest = lax.Precision.HIGHEST
    guyan_sum = jnp.dot(
        inverse_rows,
        lax.all_gather(coupling_rows, "col", axis=0, tiled=True),
        preferred_element_type=jnp.float32,
    )
    guyan = (-guyan_sum).astype(jnp.bfloat16)
    stiff_rows = boundary_stiffness[0]
    row_share = stiff_rows.shape[0]
    row_offset = column_index * row_share
    stiff_part = jnp.einsum("rb,rc->bc", coupling_rows, guyan, preferred_element_type=jnp.float32)
    stiff_part = lax.dynamic_update_slice_in_dim(
        stiff_part,
        lax.dynamic_slice_in_dim(stiff_part, row_offset, row_share, 0) + stiff_rows,
        row_offset,
        0,
    )
    weighted = (interior_mass[0][:, None] * guyan.astype(jnp.float32)).astype(jnp.bfloat16)
    mass_part = jnp.einsum("rb,rc->bc", guyan, weighted, preferred_element_type=jnp.float32)
    diagonal_rows = jnp.where(
        jnp.arange(boundary_width, dtype=jnp.int32)[None, :]
        == (row_offset + jnp.arange(row_share, dtype=jnp.int32))[:, None],
        boundary_mass[0][:, None],
        0.0,
    )
    mass_part = lax.dynamic_update_slice_in_dim(
        mass_part,
        lax.dynamic_slice_in_dim(mass_part, row_offset, row_share, 0) + diagonal_rows,
        row_offset,
        0,
    )
    previous_trial = shifted(trial_vectors, "sub", 1)
    candidates = jnp.concatenate([trial_vectors, previous_trial], axis=1)
    labels = jnp.stack([sub_index, sub_index + sub_count, previous_sub, previous_sub + sub_count])
    own_map = block_map[0]
    chooser = (own_map[:, None] == labels[None, :]).astype(jnp.bfloat16)
    local_trial = (
        jnp.einsum("tkb,ik->tib", candidates, chooser, preferred_element_type=jnp.float32)
        .astype(jnp.bfloat16)
        .reshape(trial_vectors.shape[0], boundary_width)
    )
    projected = jnp.einsum("rj,tj->tr", weighted, local_trial, preferred_element_type=jnp.float32)
    small_part = jnp.einsum(
        "tr,mr->tm", projected, interior_modes[0].astype(jnp.float32), precision=highest
    )
    stiffness, mass_sum, small_sum = lax.psum((stiff_part, mass_part, small_part), "col")
    stiff_blocks = stiffness.reshape(block_count, block_size, block_count, block_size)
    mass_blocks = mass_sum.reshape(block_count, block_size, block_count, block_size)
    row_cycles = jnp.arange(2, dtype=jnp.int32)

    def rows_for(owner_row):
        return (own_map[None, :] == row_cycles[:, None] * sub_count + owner_row).astype(jnp.float32)

    placement = (
        own_map[:, None]
        == jnp.arange(cycles, dtype=jnp.int32)[None, :] * grid_columns + column_index
    ).astype(jnp.float32)

    def select_rows(selection, blocks):
        return jnp.einsum("ri,ixjy->rxjy", selection, blocks, precision=highest)

    def spread(panel, where):
        return jnp.einsum("rxjy,jc->rxcy", panel, where, precision=highest)

    own_selection = rows_for(sub_index)
    own_stiff = spread(select_rows(own_selection, stiff_blocks), placement)
    own_mass = spread(select_rows(own_selection, mass_blocks), placement)
    leaving = rows_for(previous_sub)
    leaving_stiff = select_rows(leaving, stiff_blocks)
    leaving_mass = select_rows(leaving, mass_blocks)
    neighbour_stiff, neighbour_mass, neighbour_place = shifted(
        (leaving_stiff, leaving_mass, placement), "sub", -1
    )
    reduced_stiffness = (own_stiff + spread(neighbour_stiff, neighbour_place)).astype(jnp.bfloat16)
    reduced_mass = (own_mass + spread(neighbour_mass, neighbour_place)).astype(jnp.bfloat16)
    return (reduced_stiffness, reduced_mass, small_sum[None])


def solution(mesh):
    placed = (
        P("sub", "col", None),
        P("sub", "col", None),
        P("sub", "col", None),
        P("sub", "col"),
        P("sub", "col"),
        P("sub", None, "col"),
        P("sub", None),
        P(None, None, "sub"),
    )
    return jax.shard_map(
        shards,
        mesh=mesh,
        in_specs=placed,
        out_specs=(P(None, "sub", None, "col"), P(None, "sub", None, "col"), P("sub", None, None)),
        check_vma=False,
    )
```

profile of v0, /device:TPU:0, one launch (start us, length us, event | category | flops | bytes accessed | tf_op | source)
XLA Modules:
  0.0 169.7 jit_solution(14434118303685060885)
XLA Ops:
  7.2 0.7 all-gather.3.cloned.1.call-update
  8.0 2.0 %copy.11 = f32[1,256,512]{1,2,0:T(8,128)} copy(f32[1,256,512]{2,1,0:T(8,128)} %param.10) | data formatting | bytes 1048576 | tf_op args[2]
  10.1 47.1 %all-gather.3.cloned.1.call-done = bf16[1,3072,512]{2,1,0:T(8,128)(2,1)} async-done(((bf16[1,1536,512]{2,1,0:T(8,128)(2,1)}), bf16[1,3072,512]{2,1,0:T(8,128)(2,1)}) %all-gather.3.cloned.1.call-update) | async-done | bytes 3145744 | tf_op jit(solution)/shard_map/all_gather | solution.py:37
  57.2 9.4 %fusion.6 = bf16[1536,512]{1,0:T(8,128)(2,1)S(1)} fusion(bf16[1,3072,512]{2,1,0:T(8,128)(2,1)} %all-gather.3.cloned.1.call-done, bf16[1,1536,3072]{2,1,0:T(8,128)(2,1)} %param.8), kind=kOutput, calls=%fused_computation.5 | convolution fusion | flops 4833411072 | bytes 14155776 | tf_op jit(solution)/shard_map/dot_general | solution.py:35
  66.7 1.0 fusion.13
  67.7 0.2 copy-done.2
  67.8 1.1 fusion.12
  69.0 0.2 add_dynamic-update-slice_fusion
  69.2 1.3 reshape.41
  70.5 1.0 copy-done.5
  71.6 1.3 reshape.40
  73.1 3.5 %collective-permute-start = (f32[4,16]{1,0:T(4,128)S(1)}, f32[4,16]{1,0:T(4,128)S(1)}, u32[]{:S(2)}, u32[]{:S(2)}) collective-permute-start(f32[4,16]{1,0:T(4,128)S(1)} %compare_convert_fusion), channel_id=1, source_target_pairs={{2,0},{4,2},{6,4},{8,6},{10,8},{12,10},{14,12},{16,14},{18,16},{20... | collective-permute-start | bytes 776 | tf_op jit(solution)/shard_map/ppermute | solution.py:10
  76.7 5.9 %collective-permute-done.3 = bf16[64,2,128]{2,1,0:T(2,128)(2,1)S(1)} collective-permute-done((bf16[64,2,128]{2,1,0:T(2,128)(2,1)S(1)}, bf16[64,2,128]{2,1,0:T(2,128)(2,1)S(1)}, u32[]{:S(2)}, u32[]{:S(2)}) %collective-permute-start.3) | collective-permute-done | bytes 32800 | tf_op jit(solution)/shard_map/ppermute | solution.py:10
  82.6 0.2 convolution_convert_fusion
  82.9 0.7 fusion.11
  83.5 0.7 convolution_bitcast_fusion
  84.3 10.1 %psum.23 = f32[1,64,200]{2,1,0:T(8,128)} all-reduce(f32[1,64,200]{2,1,0:T(8,128)S(1)} %convolution_bitcast_fusion), channel_id=1, replica_groups=mesh['sub'=16,'col'=2] {'col'}, use_global_device_ids=true, to_apply=%region_2.3 | all-reduce | flops 12800 | bytes 102400 | tf_op jit(solution)/shard_map/psum | solution.py:79
  94.4 43.1 %all-reduce.3.cloned.1.call-done = (f32[4,128,4,128]{1,0,3,2:T(4,128)}, f32[4,128,4,128]{3,2,1,0:T(4,128)}) async-done(((f32[4,128,4,128]{1,0,3,2:T(4,128)}, f32[4,128,4,128]{3,2,1,0:T(4,128)}), (f32[4,128,4,128]{1,0,3,2:T(4,128)}, f32[4,128,4,128]{3,2,1,0:T(4,128)})) %all-reduce.3.cloned.1.call-update) | async-done | bytes 2097168 | tf_op jit(solution)/shard_map/psum | solution.py:79
  137.5 1.7 copy.13
  139.2 1.1 fusion.38
  140.3 0.1 copy.17
  140.5 1.7 fusion.19
  142.2 1.7 fusion.21
  144.0 3.6 %collective-permute-start.2 = (f32[2,128,4,128]{3,2,1,0:T(4,128)S(1)}, f32[2,128,4,128]{3,2,1,0:T(4,128)S(1)}, u32[]{:S(2)}, u32[]{:S(2)}) collective-permute-start(f32[2,128,4,128]{3,2,1,0:T(4,128)S(1)} %copy.21), channel_id=1, source_target_pairs={{2,0},{4,2},{6,4},{8,6},{10,8},{12,10},{14,12},{16,14},{18,16},{20... | collective-permute-start | bytes 1572872 | tf_op jit(solution)/shard_map/ppermute | solution.py:10
  147.5 0.8 collective-permute-start.1
  148.4 1.2 fusion.25
  149.6 1.1 fusion.43
  150.7 1.2 fusion.27
  151.9 2.4 %collective-permute-done.2 = f32[2,128,4,128]{3,2,1,0:T(4,128)S(1)} collective-permute-done((f32[2,128,4,128]{3,2,1,0:T(4,128)S(1)}, f32[2,128,4,128]{3,2,1,0:T(4,128)S(1)}, u32[]{:S(2)}, u32[]{:S(2)}) %collective-permute-start.2) | collective-permute-done | bytes 524320 | tf_op jit(solution)/shard_map/ppermute | solution.py:10
  154.2 3.0 %fusion.18 = bf16[2,128,16,128]{3,2,1,0:T(8,128)(2,1)} fusion(f32[16,2,128,128]{3,0,2,1:T(8,128)S(1)} %fusion.25, f32[2,128,4,128]{3,2,1,0:T(4,128)S(1)} %collective-permute-done.2, f32[4,16]{1,0:T(4,128)S(1)} %collective-permute-done), kind=kOutput, calls=%fused_computation.15 | convolution fusion | flops 26214400 | bytes 3670272 | tf_op jit(solution)/shard_map/rxjy,jc->rxcy/dot_general | solution.py:96
  157.2 2.6 %collective-permute-done.1 = f32[2,128,4,128]{3,2,1,0:T(4,128)S(1)} collective-permute-done((f32[2,128,4,128]{3,2,1,0:T(4,128)S(1)}, f32[2,128,4,128]{3,2,1,0:T(4,128)S(1)}, u32[]{:S(2)}, u32[]{:S(2)}) %collective-permute-start.1) | collective-permute-done | bytes 524320 | tf_op jit(solution)/shard_map/ppermute | solution.py:10
  159.9 3.0 %fusion.17 = bf16[2,128,16,128]{3,2,1,0:T(8,128)(2,1)} fusion(f32[16,2,128,128]{3,0,2,1:T(8,128)S(1)} %fusion.27, f32[2,128,4,128]{3,2,1,0:T(4,128)S(1)} %collective-permute-done.1, f32[4,16]{1,0:T(4,128)S(1)} %collective-permute-done), kind=kOutput, calls=%fused_computation.14 | convolution fusion | flops 26214400 | bytes 3670272 | tf_op jit(solution)/shard_map/rxjy,jc->rxcy/dot_general | solution.py:96
  (33 shorter events, 0.6 us)
Async XLA Ops:
  7.2 76.4 %copy-start = (bf16[1,200,1536]{2,1,0:T(8,128)(2,1)S(1)}, bf16[1,200,1536]{2,1,0:T(8,128)(2,1)}, u32[]{:S(2)}) copy-start(bf16[1,200,1536]{2,1,0:T(8,128)(2,1)} %param.13) | copy-start | bytes 1843204
  7.2 2.8 %copy-start.7 = (f32[1,1536]{1,0:T(1,128)S(1)}, f32[1,1536]{1,0:T(1,128)}, u32[]{:S(2)}) copy-start(f32[1,1536]{1,0:T(1,128)} %param.11) | copy-start | bytes 18436
  7.2 50.0 %all-gather.3.cloned.1.call-start = ((), (), s32[]{:S(2)}) async-start(), calls=%async_computation | async-start | bytes 4718592 | tf_op jit(solution)/shard_map/all_gather | solution.py:37
  7.9 129.6 %all-reduce.3.cloned.1.call-start = ((), (), s32[]{:S(2)}) async-start(), calls=%async_computation.1 | async-start | bytes 4194304 | tf_op jit(solution)/shard_map/psum | solution.py:79
  10.1 56.6 %copy-start.1 = (bf16[1,1536,512]{2,1,0:T(8,128)(2,1)S(1)}, bf16[1,1536,512]{2,1,0:T(8,128)(2,1)}, u32[]{:S(2)}) copy-start(bf16[1,1536,512]{2,1,0:T(8,128)(2,1)} %param.9) | copy-start | bytes 4718596
  66.7 1.2 copy-start.2
  67.8 1.2 copy-start.8
  70.5 1.0 copy-start.5
  71.6 1.4 copy-start.6
  71.6 5.0 %copy-start.9 = (bf16[64,2,128]{2,1,0:T(2,128)(2,1)S(1)}, bf16[64,2,128]{2,1,0:T(2,128)(2,1)}, u32[]{:S(2)}) copy-start(bf16[64,2,128]{2,1,0:T(2,128)(2,1)} %param.15) | copy-start | bytes 98308
  71.6 11.2 %copy-start.3 = (bf16[1536,512]{1,0:T(8,128)(2,1)S(1)}, bf16[1536,512]{1,0:T(8,128)(2,1)}, u32[]{:S(2)}) copy-start(bf16[1536,512]{1,0:T(8,128)(2,1)} %copy-done.2) | copy-start | bytes 4718596
  73.1 78.8 %collective-permute-start = (f32[4,16]{1,0:T(4,128)S(1)}, f32[4,16]{1,0:T(4,128)S(1)}, u32[]{:S(2)}, u32[]{:S(2)}) collective-permute-start(f32[4,16]{1,0:T(4,128)S(1)} %compare_convert_fusion), channel_id=1, source_target_pairs={{2,0},{4,2},{6,4},{8,6},{10,8},{12,10},{14,12},{16,14},{18,16},{20... | collective-permute-start | bytes 776 | tf_op jit(solution)/shard_map/ppermute | solution.py:10
  76.6 6.0 %collective-permute-start.3 = (bf16[64,2,128]{2,1,0:T(2,128)(2,1)S(1)}, bf16[64,2,128]{2,1,0:T(2,128)(2,1)S(1)}, u32[]{:S(2)}, u32[]{:S(2)}) collective-permute-start(bf16[64,2,128]{2,1,0:T(2,128)(2,1)S(1)} %copy-done.9), channel_id=1, source_target_pairs={{30,0},{0,2},{2,4},{4,6},{6,8},{8,10},{10,12},{12,14},{14,16},{16,... | collective-permute-start | bytes 98312 | tf_op jit(solution)/shard_map/ppermute | solution.py:10
  137.5 3.0 %copy-start.4 = (f32[4,128,4,128]{3,2,1,0:T(4,128)S(1)}, f32[4,128,4,128]{3,2,1,0:T(4,128)}, u32[]{:S(2)}) copy-start(f32[4,128,4,128]{3,2,1,0:T(4,128)} %get-tuple-element.4) | copy-start | bytes 3145732
  144.0 10.3 %collective-permute-start.2 = (f32[2,128,4,128]{3,2,1,0:T(4,128)S(1)}, f32[2,128,4,128]{3,2,1,0:T(4,128)S(1)}, u32[]{:S(2)}, u32[]{:S(2)}) collective-permute-start(f32[2,128,4,128]{3,2,1,0:T(4,128)S(1)} %copy.21), channel_id=1, source_target_pairs={{2,0},{4,2},{6,4},{8,6},{10,8},{12,10},{14,12},{16,14},{18,16},{20... | collective-permute-start | bytes 1572872 | tf_op jit(solution)/shard_map/ppermute | solution.py:10
  147.5 12.3 %collective-permute-start.1 = (f32[2,128,4,128]{3,2,1,0:T(4,128)S(1)}, f32[2,128,4,128]{3,2,1,0:T(4,128)S(1)}, u32[]{:S(2)}, u32[]{:S(2)}) collective-permute-start(f32[2,128,4,128]{3,2,1,0:T(4,128)S(1)} %copy.17), channel_id=1, source_target_pairs={{2,0},{4,2},{6,4},{8,6},{10,8},{12,10},{14,12},{16,14},{18,16},{20... | collective-permute-start | bytes 1572872 | tf_op jit(solution)/shard_map/ppermute | solution.py:10
Sparse Core Ops, SparseCore 0:
  9.5 47.6 all-gather.2
  73.1 64.3 all-reduce.2
where the time goes:
time: 170 us
  waiting for transfers between devices  102 us (60%)
  matrix products  27.1 us (16%)
  between operations  14.3 us (8%)
  blocking collectives  10.1 us (6%)
  starting transfers between devices  8 us (5%)
  local copies, waits for them, and re-layouts  7.84 us (5%)
    all_gather x1, waiting for transfers between devices, shards(): lax.all_gather(coupling_rows, 'col', axis=0, tiled=True)  47.1 us
    psum x1, waiting for transfers between devices, shards(): lax.psum((stiff_part, mass_part, small_part), 'col')  43.1 us
    ppermute x4, waiting for transfers between devices, shifted(): return lax.ppermute(block, axis, route)  10.9 us
    psum x1, blocking collectives, shards(): lax.psum((stiff_part, mass_part, small_part), 'col')  10.1 us
    dot_general x1, matrix products, shards(): jnp.dot(inverse_rows, lax.all_gather(coupling_rows, 'col', axis=0, tiled=...  9.45 us
    dot_general x4, matrix products, spread(): return jnp.einsum('rxjy,jc->rxcy', panel, where, precision=highest)  8.34 us
    ppermute x4, starting transfers between devices, shifted(): return lax.ppermute(block, axis, route)  7.92 us
    dot_general x4, matrix products, select_rows(): return jnp.einsum('ri,ixjy->rxjy', selection, blocks, precision=highest)  5.56 us
  transfers between devices with their start and end apart: 6, of which 5 were waited for; matrix products, arithmetic and copies ran while one was open for 10% of the time, Pallas kernels for 0%

commit v1 on v0

--- a/solution.py
+++ b/solution.py
@@ -1,6 +1,9 @@
+import functools
 import jax
 import jax.numpy as jnp
 from jax import lax
+from jax.experimental import pallas as pl
+from jax.experimental.pallas import tpu as pltpu
 from jax.sharding import PartitionSpec as P
 
 
@@ -109,6 +112,454 @@
     return (reduced_stiffness, reduced_mass, small_sum[None])
 
 
+def class_table(own_map, sub_index, column_index, sub_count):
+    cycle = own_map // sub_count
+    parity = own_map % 2
+    slots = jnp.arange(4, dtype=jnp.int32)
+    wanted_parity = jnp.where(slots < 2, column_index, 1 - column_index)
+    hit = (parity[None, :] == wanted_parity[:, None]) & (cycle[None, :] == (slots % 2)[:, None])
+    places = jnp.sum(jnp.where(hit, slots[None, :], 0), axis=1)
+    is_even = (sub_index % 2 == column_index).astype(jnp.int32)
+    return jnp.concatenate([places, jnp.stack([column_index, is_even])]).astype(jnp.int32)
+
+
+def pick_kernel(table_ref, source_ref, out_ref):
+    out_ref[...] = source_ref[...]
+
+
+def pick_columns(table, rows, offset, block):
+    depth = rows.shape[0]
+    return pl.pallas_call(
+        pick_kernel,
+        grid_spec=pltpu.PrefetchScalarGridSpec(
+            num_scalar_prefetch=1,
+            grid=(2,),
+            in_specs=[pl.BlockSpec((depth, block), lambda p, t: (0, t[offset + p]))],
+            out_specs=pl.BlockSpec((depth, block), lambda p, t: (0, p)),
+        ),
+        out_shape=jax.ShapeDtypeStruct((depth, 2 * block), rows.dtype),
+        cost_estimate=cost(0, 4 * depth * block * 2),
+    )(table, rows)
+
+
+def cost(flops, moved):
+    return pl.CostEstimate(flops=int(flops), bytes_accessed=int(moved), transcendentals=0)
+
+
+def tdot(a, b):
+    return lax.dot_general(a, b, (((0,), (0,)), ((), ())), preferred_element_type=jnp.float32)
+
+
+def ndot(a, b):
+    return jnp.dot(a, b, preferred_element_type=jnp.float32)
+
+
+def rdot(a, b):
+    return lax.dot_general(a, b, (((1,), (1,)), ((), ())), preferred_element_type=jnp.float32)
+
+
+def edge_block(table_ref, edge_ref, row_slot, column_slot, block):
+    local = table_ref[row_slot] - 2 * table_ref[4]
+    inside = (local >= 0) & (local < 2)
+    row = pl.multiple_of(jnp.clip(local, 0, 1) * block, block)
+    column = pl.multiple_of(table_ref[column_slot] * block, block)
+    return jnp.where(inside, edge_ref[pl.ds(row, block), pl.ds(column, block)], 0.0)
+
+
+def edge_panel(table_ref, edge_ref, row_base, column_base, block):
+    return jnp.concatenate(
+        [
+            jnp.concatenate(
+                [
+                    edge_block(table_ref, edge_ref, row_base + p, column_base + k, block)
+                    for k in range(2)
+                ],
+                axis=1,
+            )
+            for p in range(2)
+        ],
+        axis=0,
+    )
+
+
+def edge_diagonal(table_ref, weight_ref, base, block):
+    width = 2 * block
+    rows = lax.broadcasted_iota(jnp.int32, (width, width), 0)
+    columns = lax.broadcasted_iota(jnp.int32, (width, width), 1)
+    parts = []
+    for p in range(2):
+        local = table_ref[base + p] - 2 * table_ref[4]
+        inside = (local >= 0) & (local < 2)
+        parts.append(jnp.where(inside, weight_ref[pl.ds(jnp.clip(local, 0, 1), 1), :], 0.0))
+    return jnp.where(rows == columns, jnp.concatenate(parts, axis=1), 0.0)
+
+
+def scaled(mass, g):
+    half = mass.shape[1]
+    wide = g.astype(jnp.float32)
+    return jnp.concatenate([wide[:, :half] * mass, wide[:, half:] * mass], axis=1).astype(jnp.bfloat16)
+
+
+def first_kernel(
+    block,
+    table_ref,
+    near_ref,
+    far_ref,
+    mine_ref,
+    theirs_ref,
+    got_ref,
+    mass_ref,
+    edge_ref,
+    weight_ref,
+    g_ref,
+    w_ref,
+    pre_ref,
+    low_ref,
+    high_ref,
+    square_ref,
+    stiff_acc,
+    mass_acc,
+):
+    step = pl.program_id(0)
+    depth = near_ref.shape[0]
+    near = near_ref[...]
+    g = (-(ndot(near, theirs_ref[...]) + ndot(far_ref[...], got_ref[...]))).astype(jnp.bfloat16)
+    w = scaled(mass_ref[...], g)
+    g_ref[...] = g
+    w_ref[...] = w
+    pre_ref[...] = ndot(near, mine_ref[...])
+    here = pl.ds(pl.multiple_of(step * depth, depth), depth)
+
+    @pl.when(step == 0)
+    def _():
+        stiff_acc[...] = jnp.zeros_like(stiff_acc)
+        mass_acc[...] = jnp.zeros_like(mass_acc)
+
+    stiff_acc[0] += tdot(theirs_ref[here, :], g)
+    stiff_acc[1] += tdot(mine_ref[here, :], g)
+    mass_acc[...] += tdot(g, w)
+
+    @pl.when(step == pl.num_programs(0) - 1)
+    def _():
+        even = table_ref[5] == 1
+        of_theirs = (stiff_acc[0] + edge_panel(table_ref, edge_ref, 2, 2, block)).astype(jnp.bfloat16)
+        of_mine = (stiff_acc[1] + edge_panel(table_ref, edge_ref, 0, 2, block)).astype(jnp.bfloat16)
+        low_ref[...] = jnp.where(even, of_theirs, of_mine)
+        high_ref[...] = jnp.where(even, of_mine, of_theirs)
+        square_ref[...] = (mass_acc[...] + edge_diagonal(table_ref, weight_ref, 2, block)).astype(
+            jnp.bfloat16
+        )
+
+
+def second_kernel(
+    table_ref,
+    far_ref,
+    got_ref,
+    pre_ref,
+    other_w_ref,
+    mass_ref,
+    square_ref,
+    modes_ref,
+    trial_mine_ref,
+    trial_theirs_ref,
+    g_ref,
+    w_ref,
+    low_ref,
+    high_ref,
+    mass_acc,
+    small_acc,
+):
+    step = pl.program_id(0)
+    g = (-(pre_ref[...] + ndot(far_ref[...], got_ref[...]))).astype(jnp.bfloat16)
+    w = scaled(mass_ref[...], g)
+    g_ref[...] = g
+    w_ref[...] = w
+    other = other_w_ref[...]
+
+    @pl.when(step == 0)
+    def _():
+        mass_acc[...] = jnp.zeros_like(mass_acc)
+        small_acc[...] = jnp.zeros_like(small_acc)
+
+    mass_acc[...] += tdot(g, other)
+    projected = rdot(trial_mine_ref[...], w) + rdot(trial_theirs_ref[...], other)
+    upper = projected.astype(jnp.bfloat16)
+    lower = (projected - upper.astype(jnp.float32)).astype(jnp.bfloat16)
+    modes = modes_ref[...]
+    small_acc[...] += rdot(upper, modes) + rdot(lower, modes)
+
+    @pl.when(step == pl.num_programs(0) - 1)
+    def _():
+        even = table_ref[5] == 1
+        mixed = mass_acc[...].astype(jnp.bfloat16)
+        square = square_ref[...]
+        width = square.shape[0]
+        low_ref[...] = jnp.where(even, square, mixed)
+        high_ref[pl.ds(0, width), :] = jnp.where(even, mixed, square)
+        small = small_acc[...]
+        count, modes_count = small.shape
+        high_ref[pl.ds(width, count), :] = jnp.concatenate(
+            [small, jnp.zeros((count, width - modes_count), jnp.float32)], axis=1
+        ).astype(jnp.bfloat16)
+
+
+def third_kernel(
+    block,
+    table_ref,
+    g_ref,
+    w_ref,
+    other_g_ref,
+    mine_ref,
+    theirs_ref,
+    edge_ref,
+    weight_ref,
+    low_ref,
+    high_ref,
+    acc,
+):
+    step = pl.program_id(0)
+
+    @pl.when(step == 0)
+    def _():
+        acc[...] = jnp.zeros_like(acc)
+
+    g = g_ref[...]
+    w = w_ref[...]
+    acc[0] += tdot(theirs_ref[...], g)
+    acc[1] += tdot(mine_ref[...], g)
+    acc[2] += tdot(other_g_ref[...], w)
+    acc[3] += tdot(g, w)
+
+    @pl.when(step == pl.num_programs(0) - 1)
+    def _():
+        even = table_ref[5] == 1
+        stiff_theirs = acc[0] + edge_panel(table_ref, edge_ref, 2, 0, block)
+        stiff_mine = acc[1] + edge_panel(table_ref, edge_ref, 0, 0, block)
+        mass_theirs = acc[2]
+        mass_mine = acc[3] + edge_diagonal(table_ref, weight_ref, 0, block)
+        low_ref[0] = jnp.where(even, stiff_theirs, stiff_mine).astype(jnp.bfloat16)
+        low_ref[1] = jnp.where(even, mass_theirs, mass_mine).astype(jnp.bfloat16)
+        high_ref[0] = jnp.where(even, stiff_mine, stiff_theirs)
+        high_ref[1] = jnp.where(even, mass_mine, mass_theirs)
+
+
+def place_kernel(block, spots_ref, own_ref, high_ref, low_ref, cross_ref, out_ref):
+    kept = own_ref[0] + high_ref[...].astype(jnp.float32)
+    moved = low_ref[0].astype(jnp.float32) + cross_ref[...].astype(jnp.float32)
+    count, cycles = out_ref.shape[1], out_ref.shape[2]
+    lanes = lax.broadcasted_iota(jnp.int32, (count, cycles, block), 1)
+    total = jnp.zeros((count, cycles, block), jnp.float32)
+    for k in range(2):
+        part = slice(k * block, (k + 1) * block)
+        total += jnp.where(lanes == spots_ref[k], kept[:, part][:, None, :], 0.0)
+        total += jnp.where(lanes == spots_ref[2 + k], moved[:, part][:, None, :], 0.0)
+    out_ref[0] = total.astype(out_ref.dtype)
+
+
+def place(spots, own, high, low, cross, which, cycles, block):
+    width = 2 * block
+    rows = min(64, block)
+    steps = block // rows
+    flat = lambda p, x, t: (p * steps + x, 0)
+    deep = lambda p, x, t: (which, p * steps + x, 0)
+    return pl.pallas_call(
+        functools.partial(place_kernel, block),
+        grid_spec=pltpu.PrefetchScalarGridSpec(
+            num_scalar_prefetch=1,
+            grid=(2, steps),
+            in_specs=[
+                pl.BlockSpec((1, rows, width), deep),
+                pl.BlockSpec((rows, width), flat),
+                pl.BlockSpec((1, rows, width), deep),
+                pl.BlockSpec((rows, width), flat),
+            ],
+            out_specs=pl.BlockSpec((1, rows, cycles, block), lambda p, x, t: (p, x, 0, 0)),
+        ),
+        out_shape=jax.ShapeDtypeStruct((2, block, cycles, block), jnp.bfloat16),
+        cost_estimate=cost(2 * block * cycles * block * 8, 4 * block * cycles * block),
+    )(spots, own, high, low, cross)
+
+
+def pair_shards(
+    interior_inverse,
+    interface_coupling,
+    boundary_stiffness,
+    interior_mass,
+    boundary_mass,
+    interior_modes,
+    block_map,
+    trial_vectors,
+):
+    inverse_rows = interior_inverse[0]
+    coupling_rows = interface_coupling[0]
+    edge = boundary_stiffness[0]
+    depth, _ = inverse_rows.shape
+    block = trial_vectors.shape[2]
+    width = 2 * block
+    trials = trial_vectors.shape[0]
+    modes = interior_modes[0]
+    modes_count = modes.shape[0]
+    sub_count = lax.axis_size("sub")
+    sub_index = lax.axis_index("sub")
+    column_index = lax.axis_index("col")
+    cycles = 2 * sub_count // 2
+    table = class_table(block_map[0], sub_index, column_index, sub_count)
+    even = table[5] == 1
+    swap = [(0, 1), (1, 0)]
+    both = ("sub", "col")
+    back = [(i, (i - 1) % sub_count) for i in range(sub_count)]
+    cross = [
+        (2 * i + c, 2 * ((i - 1) % sub_count) + 1 - c) for i in range(sub_count) for c in range(2)
+    ]
+    mine = pick_columns(table, coupling_rows, 0, block)
+    got_theirs = lax.ppermute(mine, "col", swap)
+    theirs = pick_columns(table, coupling_rows, 2, block)
+    got_mine = lax.ppermute(theirs, "col", swap)
+    previous_trial = shifted(trial_vectors, "sub", 1)
+    trial_high = trial_vectors.reshape(trials, width)
+    trial_low = previous_trial.reshape(trials, width)
+    trial_mine = jnp.where(even, trial_high, trial_low)
+    trial_theirs = jnp.where(even, trial_low, trial_high)
+    mass_columns = jnp.broadcast_to(interior_mass[0][:, None], (depth, block))
+    weights = boundary_mass[0].reshape(2, block)
+
+    tile = depth // 3
+    steps = 3
+    row = lambda i, t: (i, 0)
+    whole = lambda i, t: (0, 0)
+    bf16, f32 = jnp.bfloat16, jnp.float32
+    arbitrary = pltpu.CompilerParams(dimension_semantics=("arbitrary",))
+    g_theirs, w_theirs, pre, stiff_low, stiff_high, square = pl.pallas_call(
+        functools.partial(first_kernel, block),
+        grid_spec=pltpu.PrefetchScalarGridSpec(
+            num_scalar_prefetch=1,
+            grid=(steps,),
+            in_specs=[
+                pl.BlockSpec((tile, depth), lambda i, t: (i, t[4])),
+                pl.BlockSpec((tile, depth), lambda i, t: (i, 1 - t[4])),
+                pl.BlockSpec((depth, width), whole),
+                pl.BlockSpec((depth, width), whole),
+                pl.BlockSpec((depth, width), whole),
+                pl.BlockSpec((tile, block), row),
+                pl.BlockSpec(edge.shape, whole),
+                pl.BlockSpec(weights.shape, whole),
+            ],
+            out_specs=[
+                pl.BlockSpec((tile, width), row),
+                pl.BlockSpec((tile, width), row),
+                pl.BlockSpec((tile, width), row),
+                pl.BlockSpec((width, width), whole),
+                pl.BlockSpec((width, width), whole),
+                pl.BlockSpec((width, width), whole),
+            ],
+            scratch_shapes=[pltpu.VMEM((2, width, width), f32), pltpu.VMEM((width, width), f32)],
+        ),
+        out_shape=[
+            jax.ShapeDtypeStruct((depth, width), bf16),
+            jax.ShapeDtypeStruct((depth, width), bf16),
+            jax.ShapeDtypeStruct((depth, width), f32),
+            jax.ShapeDtypeStruct((width, width), bf16),
+            jax.ShapeDtypeStruct((width, width), bf16),
+            jax.ShapeDtypeStruct((width, width), bf16),
+        ],
+        compiler_params=arbitrary,
+        cost_estimate=cost(6 * depth * depth * width, 4 * depth * depth),
+        name="first",
+    )(table, inverse_rows, inverse_rows, mine, theirs, got_theirs, mass_columns, edge, weights)
+    cross_stiff = lax.ppermute(stiff_low, both, cross)
+    high_stiff = lax.ppermute(stiff_high, "col", swap)
+
+    g_mine, w_mine, mass_low, mass_high = pl.pallas_call(
+        second_kernel,
+        grid_spec=pltpu.PrefetchScalarGridSpec(
+            num_scalar_prefetch=1,
+            grid=(steps,),
+            in_specs=[
+                pl.BlockSpec((tile, depth), lambda i, t: (i, 1 - t[4])),
+                pl.BlockSpec((depth, width), whole),
+                pl.BlockSpec((tile, width), row),
+                pl.BlockSpec((tile, width), row),
+                pl.BlockSpec((tile, block), row),
+                pl.BlockSpec((width, width), whole),
+                pl.BlockSpec((modes_count, tile), lambda i, t: (0, i)),
+                pl.BlockSpec((trials, width), whole),
+                pl.BlockSpec((trials, width), whole),
+            ],
+            out_specs=[
+                pl.BlockSpec((tile, width), row),
+                pl.BlockSpec((tile, width), row),
+                pl.BlockSpec((width, width), whole),
+                pl.BlockSpec((width + trials, width), whole),
+            ],
+            scratch_shapes=[
+                pltpu.VMEM((width, width), f32),
+                pltpu.VMEM((trials, modes_count), f32),
+            ],
+        ),
+        out_shape=[
+            jax.ShapeDtypeStruct((depth, width), bf16),
+            jax.ShapeDtypeStruct((depth, width), bf16),
+            jax.ShapeDtypeStruct((width, width), bf16),
+            jax.ShapeDtypeStruct((width + trials, width), bf16),
+        ],
+        compiler_params=arbitrary,
+        cost_estimate=cost(2 * depth * depth * width, 2 * depth * depth),
+        name="second",
+    )(
+        table,
+        inverse_rows,
+        got_mine,
+        pre,
+        w_theirs,
+        mass_columns,
+        square,
+        modes,
+        trial_mine,
+        trial_theirs,
+    )
+    high_mass = lax.ppermute(mass_high, "col", swap)
+    cross_mass = lax.ppermute(mass_low, both, cross)
+
+    low, own = pl.pallas_call(
+        functools.partial(third_kernel, block),
+        grid_spec=pltpu.PrefetchScalarGridSpec(
+            num_scalar_prefetch=1,
+            grid=(steps,),
+            in_specs=[
+                pl.BlockSpec((tile, width), row),
+                pl.BlockSpec((tile, width), row),
+                pl.BlockSpec((tile, width), row),
+                pl.BlockSpec((tile, width), row),
+                pl.BlockSpec((tile, width), row),
+                pl.BlockSpec(edge.shape, whole),
+                pl.BlockSpec(weights.shape, whole),
+            ],
+            out_specs=[
+                pl.BlockSpec((2, width, width), lambda i, t: (0, 0, 0)),
+                pl.BlockSpec((2, width, width), lambda i, t: (0, 0, 0)),
+            ],
+            scratch_shapes=[pltpu.VMEM((4, width, width), f32)],
+        ),
+        out_shape=[
+            jax.ShapeDtypeStruct((2, width, width), bf16),
+            jax.ShapeDtypeStruct((2, width, width), f32),
+        ],
+        compiler_params=arbitrary,
+        cost_estimate=cost(8 * depth * width * width, 10 * depth * width),
+        name="third",
+    )(table, g_mine, w_mine, g_theirs, mine, theirs, edge, weights)
+    low_here = lax.ppermute(low, "sub", back)
+
+    high_base = jnp.where(even, sub_index, (sub_index + sub_count - 1) % sub_count)
+    low_base = jnp.where(even, sub_index, (sub_index + 1) % sub_count)
+    bases = jnp.stack([high_base, high_base + sub_count, low_base, low_base + sub_count])
+    spots = (bases // 2).astype(jnp.int32)
+    reduced_stiffness = place(spots, own, high_stiff, low_here, cross_stiff, 0, cycles, block)
+    reduced_mass = place(spots, own, high_mass, low_here, cross_mass, 1, cycles, block)
+    small = mass_high[width:, :modes_count].astype(f32) + high_mass[width:, :modes_count].astype(f32)
+    return (reduced_stiffness, reduced_mass, small[None])
+
+
 def solution(mesh):
     placed = (
         P("sub", "col", None),
@@ -120,8 +571,9 @@
         P("sub", None),
         P(None, None, "sub"),
     )
+    paired = mesh.shape["col"] == 2 and mesh.shape["sub"] % 2 == 0
     return jax.shard_map(
-        shards,
+        pair_shards if paired else shards,
         mesh=mesh,
         in_specs=placed,
         out_specs=(P(None, "sub", None, "col"), P(None, "sub", None, "col"), P("sub", None, None)),

time: 170 us -> 82.9 us (0.49)
  waiting for transfers between devices: 102 us -> 21.7 us
  Pallas kernels: 0 us -> 40.6 us
  matrix products: 27.1 us -> 0 us
  between operations: 14.3 us -> 0.73 us
  blocking collectives: 10.1 us -> 0 us
  local copies, waits for them, and re-layouts: 7.84 us -> 4.7 us
  other arithmetic: 0.43 us -> 3.47 us
  starting transfers between devices: 8 us -> 11 us
    all_gather x1 -> x0, waiting for transfers between devices: 47.1 us -> none  [shards(): lax.all_gather(coupling_rows, 'col', axis=0, tiled=True)]
    psum x1 -> x0, waiting for transfers between devices: 43.1 us -> none  [shards(): lax.psum((stiff_part, mass_part, small_part), 'col')]
    pallas_call x0 -> x7, Pallas kernels: none -> 40.6 us  [the longest x1 11.9 us: pair_shards(): pl.pallas_call(functools.partial(first_kernel, block), grid_spec=pltpu.Pr...]
    dot_general x14 -> x0, matrix products: 27.1 us -> none  [the longest x1 9.45 us: shards(): jnp.dot(inverse_rows, lax.all_gather(coupling_rows, 'col', axis=0, tiled=...]
    ppermute x0 -> x7, waiting for transfers between devices: none -> 18.3 us  [the longest x1 11.9 us: pair_shards(): got_theirs = lax.ppermute(mine, 'col', swap)]
    ppermute x0 -> x7, starting transfers between devices: none -> 11 us  [the longest x1 2.97 us: pair_shards(): got_theirs = lax.ppermute(mine, 'col', swap)]
    psum x1 -> x0, blocking collectives: 10.1 us -> none  [shards(): lax.psum((stiff_part, mass_part, small_part), 'col')]
    ppermute x4 -> x1, starting transfers between devices: 7.92 us -> 0.01 us  [shifted(): return lax.ppermute(block, axis, route)]
  transfers between devices with their start and end apart: 6 -> 8, of which waited for: 5 -> 4; matrix products, arithmetic and copies ran while one was open for 10% -> 5% of each run, Pallas kernels for 0% -> 30%
where the time goes in v1:
time: 82.9 us; the launch traced here: 82.2 us
  Pallas kernels  40.6 us (49%)
  waiting for transfers between devices  21.7 us (26%)
  starting transfers between devices  11 us (13%)
  local copies, waits for them, and re-layouts  4.7 us (6%)
  other arithmetic  3.47 us (4%)
    ppermute x1, waiting for transfers between devices, pair_shards(): got_theirs = lax.ppermute(mine, 'col', swap)  11.9 us
    pallas_call x1, Pallas kernels, pair_shards(): pl.pallas_call(functools.partial(first_kernel, block), grid_spec=pltpu.Pr...  11.9 us
    pallas_call x1, Pallas kernels, pair_shards(): pl.pallas_call(second_kernel, grid_spec=pltpu.PrefetchScalarGridSpec(num_...  9.11 us
    pallas_call x2, Pallas kernels, place(): pl.pallas_call(functools.partial(place_kernel, block), grid_spec=pltpu.Pr...  8.59 us
    pallas_call x1, Pallas kernels, pair_shards(): pl.pallas_call(functools.partial(third_kernel, block), grid_spec=pltpu.Pr...  5.77 us
    pallas_call x2, Pallas kernels, pick_columns(): pl.pallas_call(pick_kernel, grid_spec=pltpu.PrefetchScalarGridSpec(num_sc...  5.2 us
    ppermute x1, waiting for transfers between devices, pair_shards(): cross_mass = lax.ppermute(mass_low, both, cross)  3.47 us
    ppermute x1, waiting for transfers between devices, shifted(): return lax.ppermute(block, axis, route)  3.35 us
  transfers between devices with their start and end apart: 8, of which 4 were waited for; matrix products, arithmetic and copies ran while one was open for 5% of the time, Pallas kernels for 30%

profile of v1, /device:TPU:0, one launch (start us, length us, event | category | flops | bytes accessed | tf_op | source)
XLA Modules:
  0.0 82.2 jit_solution(8490658547266549557)
XLA Ops:
  0.7 0.7 fusion
  1.3 0.2 select_reduce_fusion
  1.5 0.6 pad_add_fusion.1.table_ref
  2.1 2.6 %shard_map.104.mine_ref = bf16[1536,256]{1,0:T(8,128)(2,1)} custom-call(s32[6]{0:T(128)} %pad_add_fusion.1.table_ref, bf16[1536,512]{1,0:T(8,128)(2,1)} %bitcast.30), custom_call_target="tpu_custom_call" | custom-call | bytes 1572864 | tf_op jit(solution)/shard_map/pallas_call | solution.py:132
  4.7 3.0 %collective-permute-start.1 = (bf16[1536,256]{1,0:T(8,128)(2,1)}, bf16[1536,256]{1,0:T(8,128)(2,1)S(1)}, u32[]{:S(2)}, u32[]{:S(2)}) collective-permute-start(bf16[1536,256]{1,0:T(8,128)(2,1)} %shard_map.104.mine_ref), channel_id=1, source_target_pairs={{0,1},{1,0},{2,3},{3,2},{4,5},{5,4},{6,7},{7,6},{8,9},{9,8},{10,11... | collective-permute-start | bytes 2359304 | tf_op jit(solution)/shard_map/ppermute | solution.py:415
  7.7 0.0 collective-permute-start.2
  7.7 2.6 %shard_map.103.theirs_ref = bf16[1536,256]{1,0:T(8,128)(2,1)} custom-call(s32[6]{0:T(128)} %pad_add_fusion.1.table_ref, bf16[1536,512]{1,0:T(8,128)(2,1)} %bitcast.31), custom_call_target="tpu_custom_call" | custom-call | bytes 1572864 | tf_op jit(solution)/shard_map/pallas_call | solution.py:132
  10.3 0.1 collective-permute-start
  10.4 3.4 %collective-permute-done.2 = bf16[64,2,128]{2,1,0:T(2,128)(2,1)S(1)} collective-permute-done((bf16[64,2,128]{2,1,0:T(2,128)(2,1)S(1)}, bf16[64,2,128]{2,1,0:T(2,128)(2,1)S(1)}, u32[]{:S(2)}, u32[]{:S(2)}) %collective-permute-start.2) | collective-permute-done | bytes 32800 | tf_op jit(solution)/shard_map/ppermute | solution.py:13
  13.8 0.6 copy_bitcast_fusion
  14.4 11.9 %collective-permute-done.1.got_ref = bf16[1536,256]{1,0:T(8,128)(2,1)S(1)} collective-permute-done((bf16[1536,256]{1,0:T(8,128)(2,1)}, bf16[1536,256]{1,0:T(8,128)(2,1)S(1)}, u32[]{:S(2)}, u32[]{:S(2)}) %collective-permute-start.1) | collective-permute-done | bytes 786464 | tf_op jit(solution)/shard_map/ppermute | solution.py:415
  26.3 1.2 %broadcast_in_dim.40.mass_ref = f32[1536,128]{1,0:T(8,128)} broadcast(f32[1536]{0:T(1024)S(1)} %reduce), dimensions={0} | broadcast | bytes 792576 | tf_op jit(solution)/shard_map/broadcast_in_dim | solution.py:423
  27.5 11.9 %first.1 = (bf16[1536,256]{1,0:T(8,128)(2,1)}, bf16[1536,256]{1,0:T(8,128)(2,1)}, f32[1536,256]{1,0:T(8,128)}, bf16[256,256]{1,0:T(8,128)(2,1)}, bf16[256,256]{1,0:T(8,128)(2,1)}, /*index=5*/bf16[256,256]{1,0:T(8,128)(2,1)}) custom-call(s32[6]{0:T(128)} %pad_add_fusion.1.table_ref, bf16[1536,3072]{1,0:T(8,128)(2,1)} %bitcast.27, ...), custom_call_target="tpu_custom_call" | custom-call | flops 3623878656 | bytes 9437184 | tf_op jit(solution)/shard_map/first/pallas_call | solution.py:432
  39.4 2.9 %collective-permute-done.got_ref = bf16[1536,256]{1,0:T(8,128)(2,1)S(1)} collective-permute-done((bf16[1536,256]{1,0:T(8,128)(2,1)}, bf16[1536,256]{1,0:T(8,128)(2,1)S(1)}, u32[]{:S(2)}, u32[]{:S(2)}) %collective-permute-start) | collective-permute-done | bytes 786464 | tf_op jit(solution)/shard_map/ppermute | solution.py:417
  42.3 0.9 %copy-done.2 = bf16[1536,256]{1,0:T(8,128)(2,1)} copy-done((bf16[1536,256]{1,0:T(8,128)(2,1)}, bf16[1536,256]{1,0:T(8,128)(2,1)S(1)}, u32[]{:S(2)}) %copy-start.2) | copy-done | bytes 786456
  43.2 9.1 %second.1 = (bf16[1536,256]{1,0:T(8,128)(2,1)}, bf16[1536,256]{1,0:T(8,128)(2,1)}, bf16[256,256]{1,0:T(8,128)(2,1)}, bf16[320,256]{1,0:T(8,128)(2,1)}) custom-call(s32[6]{0:T(128)} %pad_add_fusion.1.table_ref, bf16[1536,3072]{1,0:T(8,128)(2,1)} %bitcast.29, bf16[1536,256]{1,0:T(8,128)(2,1)} %copy-done.2, f32[1536,256]{1,0:T(8,128)} %get-tuple-element.15.pre_ref, ...), custom_call_target="tpu_custom_call" | custom-call | flops 1207959552 | bytes 4718592 | tf_op jit(solution)/shard_map/second/pallas_call | solution.py:472
  52.3 1.8 %collective-permute-start.6 = (bf16[320,256]{1,0:T(8,128)(2,1)}, bf16[320,256]{1,0:T(8,128)(2,1)S(1)}, u32[]{:S(2)}, u32[]{:S(2)}) collective-permute-start(bf16[320,256]{1,0:T(8,128)(2,1)} %get-tuple-element.25), channel_id=1, source_target_pairs={{0,1},{1,0},{2,3},{3,2},{4,5},{5,4},{6,7},{7,6},{8,9},{9,8},{10,11... | collective-permute-start | bytes 491528 | tf_op jit(solution)/shard_map/ppermute | solution.py:520
  54.1 5.8 %third.1 = (bf16[2,256,256]{2,1,0:T(8,128)(2,1)}, f32[2,256,256]{2,1,0:T(8,128)}) custom-call(s32[6]{0:T(128)} %pad_add_fusion.1.table_ref, bf16[1536,256]{1,0:T(8,128)(2,1)} %get-tuple-element.18.g_ref, bf16[1536,256]{1,0:T(8,128)(2,1)} %get-tuple-element.19.w_ref, bf16[1536,256]{1,0:T(8,128)(2,1)} %get-tuple-element.20.other_g_ref, ...), custom_call_target="tpu_custom_call" | custom-call | flops 805306368 | bytes 3932160 | tf_op jit(solution)/shard_map/third/pallas_call | solution.py:523
  59.9 2.9 %collective-permute-start.4 = (bf16[2,256,256]{2,1,0:T(8,128)(2,1)}, bf16[2,256,256]{2,1,0:T(8,128)(2,1)S(1)}, u32[]{:S(2)}, u32[]{:S(2)}) collective-permute-start(bf16[2,256,256]{2,1,0:T(8,128)(2,1)} %get-tuple-element.23), channel_id=1, source_target_pairs={{0,30},{2,0},{4,2},{6,4},{8,6},{10,8},{12,10},{14,12},{16,14},{18,... | collective-permute-start | bytes 786440 | tf_op jit(solution)/shard_map/ppermute | solution.py:551
  62.8 0.6 and_select_fusion.3.spots_ref
  63.3 1.8 %collective-permute-start.7 = (bf16[256,256]{1,0:T(8,128)(2,1)S(1)}, bf16[256,256]{1,0:T(8,128)(2,1)S(1)}, u32[]{:S(2)}, u32[]{:S(2)}) collective-permute-start(bf16[256,256]{1,0:T(8,128)(2,1)S(1)} %copy-done.11), channel_id=1, source_target_pairs={{0,31},{1,30},{2,1},{3,0},{4,3},{5,2},{6,5},{7,4},{8,7},{9,6},{10,... | collective-permute-start | bytes 393224 | tf_op jit(solution)/shard_map/ppermute | solution.py:521
  65.1 1.5 %collective-permute-start.3 = (bf16[256,256]{1,0:T(8,128)(2,1)S(1)}, bf16[256,256]{1,0:T(8,128)(2,1)S(1)}, u32[]{:S(2)}, u32[]{:S(2)}) collective-permute-start(bf16[256,256]{1,0:T(8,128)(2,1)S(1)} %copy-done.10), channel_id=1, source_target_pairs={{0,1},{1,0},{2,3},{3,2},{4,5},{5,4},{6,7},{7,6},{8,9},{9,8},{10,11... | collective-permute-start | bytes 393224 | tf_op jit(solution)/shard_map/ppermute | solution.py:470
  66.6 0.0 collective-permute-start.5
  66.6 1.4 %add_bitcast_fusion = f32[1,64,200]{2,1,0:T(8,128)} fusion(bf16[320,256]{1,0:T(8,128)(2,1)S(1)} %collective-permute-done.6.high_ref, bf16[320,256]{1,0:T(8,128)(2,1)} %get-tuple-element.25), kind=kLoop, calls=%fused_computation | loop fusion | flops 38400 | bytes 102400 | tf_op jit(solution)/shard_map/broadcast_in_dim | solution.py:560
  68.1 3.5 %collective-permute-done.7.cross_ref = bf16[256,256]{1,0:T(8,128)(2,1)S(1)} collective-permute-done((bf16[256,256]{1,0:T(8,128)(2,1)S(1)}, bf16[256,256]{1,0:T(8,128)(2,1)S(1)}, u32[]{:S(2)}, u32[]{:S(2)}) %collective-permute-start.7) | collective-permute-done | bytes 131104 | tf_op jit(solution)/shard_map/ppermute | solution.py:521
  71.5 0.6 copy-done.6
  72.2 0.1 copy-done
  72.3 4.3 %shard_map.106 = bf16[2,128,16,128]{3,2,1,0:T(8,128)(2,1)} custom-call(s32[4]{0:T(128)} %and_select_fusion.3.spots_ref, f32[2,256,256]{2,1,0:T(8,128)} %get-tuple-element.21.own_ref, bf16[320,256]{1,0:T(8,128)(2,1)} %copy-done.3, bf16[2,256,256]{2,1,0:T(8,128)(2,1)} %copy-done, bf16[256,256]{1,0:T(8,128)(2,1)} %copy-done.6), custom_call_target="tpu_custom_call" | custom-call | flops 4194304 | bytes 1048576 | tf_op jit(solution)/shard_map/pallas_call | solution.py:365
  76.6 0.0 collective-permute-done.5.cross_ref
  76.6 0.6 copy-done.4
  77.2 0.6 copy-done.5
  77.9 4.3 %shard_map.105 = bf16[2,128,16,128]{3,2,1,0:T(8,128)(2,1)} custom-call(s32[4]{0:T(128)} %and_select_fusion.3.spots_ref, f32[2,256,256]{2,1,0:T(8,128)} %get-tuple-element.21.own_ref, bf16[256,256]{1,0:T(8,128)(2,1)} %copy-done.4, bf16[2,256,256]{2,1,0:T(8,128)(2,1)} %copy-done, bf16[256,256]{1,0:T(8,128)(2,1)} %copy-done.5), custom_call_target="tpu_custom_call" | custom-call | flops 4194304 | bytes 1048576 | tf_op jit(solution)/shard_map/pallas_call | solution.py:365
  (25 shorter events, 0.1 us)
Async XLA Ops:
  0.6 7.1 %copy-start.7 = (bf16[64,2,128]{2,1,0:T(2,128)(2,1)S(1)}, bf16[64,2,128]{2,1,0:T(2,128)(2,1)}, u32[]{:S(2)}) copy-start(bf16[64,2,128]{2,1,0:T(2,128)(2,1)} %param.15) | copy-start | bytes 98308
  4.7 5.6 %copy-start.8 = (f32[1,1536]{1,0:T(1,128)S(1)}, f32[1,1536]{1,0:T(1,128)}, u32[]{:S(2)}) copy-start(f32[1,1536]{1,0:T(1,128)} %param.11) | copy-start | bytes 18436
  4.7 21.6 %collective-permute-start.1 = (bf16[1536,256]{1,0:T(8,128)(2,1)}, bf16[1536,256]{1,0:T(8,128)(2,1)S(1)}, u32[]{:S(2)}, u32[]{:S(2)}) collective-permute-start(bf16[1536,256]{1,0:T(8,128)(2,1)} %shard_map.104.mine_ref), channel_id=1, source_target_pairs={{0,1},{1,0},{2,3},{3,2},{4,5},{5,4},{6,7},{7,6},{8,9},{9,8},{10,11... | collective-permute-start | bytes 2359304 | tf_op jit(solution)/shard_map/ppermute | solution.py:415
  7.7 6.0 %collective-permute-start.2 = (bf16[64,2,128]{2,1,0:T(2,128)(2,1)S(1)}, bf16[64,2,128]{2,1,0:T(2,128)(2,1)S(1)}, u32[]{:S(2)}, u32[]{:S(2)}) collective-permute-start(bf16[64,2,128]{2,1,0:T(2,128)(2,1)S(1)} %copy-done.7), channel_id=1, source_target_pairs={{30,0},{0,2},{2,4},{4,6},{6,8},{8,10},{10,12},{12,14},{14,16},{16,... | collective-permute-start | bytes 98312 | tf_op jit(solution)/shard_map/ppermute | solution.py:13
  10.3 32.0 %collective-permute-start = (bf16[1536,256]{1,0:T(8,128)(2,1)}, bf16[1536,256]{1,0:T(8,128)(2,1)S(1)}, u32[]{:S(2)}, u32[]{:S(2)}) collective-permute-start(bf16[1536,256]{1,0:T(8,128)(2,1)} %shard_map.103.theirs_ref), channel_id=1, source_target_pairs={{0,1},{1,0},{2,3},{3,2},{4,5},{5,4},{6,7},{7,6},{8,9},{9,8},{10,11... | collective-permute-start | bytes 2359304 | tf_op jit(solution)/shard_map/ppermute | solution.py:417
  26.3 1.2 %copy-start.1 = (bf16[1536,256]{1,0:T(8,128)(2,1)}, bf16[1536,256]{1,0:T(8,128)(2,1)S(1)}, u32[]{:S(2)}) copy-start(bf16[1536,256]{1,0:T(8,128)(2,1)S(1)} %collective-permute-done.1.got_ref) | copy-start | bytes 2359300
  42.3 0.9 %copy-start.2 = (bf16[1536,256]{1,0:T(8,128)(2,1)}, bf16[1536,256]{1,0:T(8,128)(2,1)S(1)}, u32[]{:S(2)}) copy-start(bf16[1536,256]{1,0:T(8,128)(2,1)S(1)} %collective-permute-done.got_ref) | copy-start | bytes 2359300
  52.3 14.3 %collective-permute-start.6 = (bf16[320,256]{1,0:T(8,128)(2,1)}, bf16[320,256]{1,0:T(8,128)(2,1)S(1)}, u32[]{:S(2)}, u32[]{:S(2)}) collective-permute-start(bf16[320,256]{1,0:T(8,128)(2,1)} %get-tuple-element.25), channel_id=1, source_target_pairs={{0,1},{1,0},{2,3},{3,2},{4,5},{5,4},{6,7},{7,6},{8,9},{9,8},{10,11... | collective-permute-start | bytes 491528 | tf_op jit(solution)/shard_map/ppermute | solution.py:520
  54.1 9.2 %copy-start.11 = (bf16[256,256]{1,0:T(8,128)(2,1)S(1)}, bf16[256,256]{1,0:T(8,128)(2,1)}, u32[]{:S(2)}) copy-start(bf16[256,256]{1,0:T(8,128)(2,1)} %get-tuple-element.26) | copy-start | bytes 393220
  54.1 11.0 %copy-start.10 = (bf16[256,256]{1,0:T(8,128)(2,1)S(1)}, bf16[256,256]{1,0:T(8,128)(2,1)}, u32[]{:S(2)}) copy-start(bf16[256,256]{1,0:T(8,128)(2,1)} %get-tuple-element.22) | copy-start | bytes 393220
  54.1 12.5 %copy-start.9 = (bf16[256,256]{1,0:T(8,128)(2,1)S(1)}, bf16[256,256]{1,0:T(8,128)(2,1)}, u32[]{:S(2)}) copy-start(bf16[256,256]{1,0:T(8,128)(2,1)} %get-tuple-element.24) | copy-start | bytes 393220
  59.9 11.6 %collective-permute-start.4 = (bf16[2,256,256]{2,1,0:T(8,128)(2,1)}, bf16[2,256,256]{2,1,0:T(8,128)(2,1)S(1)}, u32[]{:S(2)}, u32[]{:S(2)}) collective-permute-start(bf16[2,256,256]{2,1,0:T(8,128)(2,1)} %get-tuple-element.23), channel_id=1, source_target_pairs={{0,30},{2,0},{4,2},{6,4},{8,6},{10,8},{12,10},{14,12},{16,14},{18,... | collective-permute-start | bytes 786440 | tf_op jit(solution)/shard_map/ppermute | solution.py:551
  63.3 8.2 %collective-permute-start.7 = (bf16[256,256]{1,0:T(8,128)(2,1)S(1)}, bf16[256,256]{1,0:T(8,128)(2,1)S(1)}, u32[]{:S(2)}, u32[]{:S(2)}) collective-permute-start(bf16[256,256]{1,0:T(8,128)(2,1)S(1)} %copy-done.11), channel_id=1, source_target_pairs={{0,31},{1,30},{2,1},{3,0},{4,3},{5,2},{6,5},{7,4},{8,7},{9,6},{10,... | collective-permute-start | bytes 393224 | tf_op jit(solution)/shard_map/ppermute | solution.py:521
  65.1 11.5 %collective-permute-start.3 = (bf16[256,256]{1,0:T(8,128)(2,1)S(1)}, bf16[256,256]{1,0:T(8,128)(2,1)S(1)}, u32[]{:S(2)}, u32[]{:S(2)}) collective-permute-start(bf16[256,256]{1,0:T(8,128)(2,1)S(1)} %copy-done.10), channel_id=1, source_target_pairs={{0,1},{1,0},{2,3},{3,2},{4,5},{5,4},{6,7},{7,6},{8,9},{9,8},{10,11... | collective-permute-start | bytes 393224 | tf_op jit(solution)/shard_map/ppermute | solution.py:470
  66.6 10.0 %collective-permute-start.5 = (bf16[256,256]{1,0:T(8,128)(2,1)S(1)}, bf16[256,256]{1,0:T(8,128)(2,1)S(1)}, u32[]{:S(2)}, u32[]{:S(2)}) collective-permute-start(bf16[256,256]{1,0:T(8,128)(2,1)S(1)} %copy-done.9), channel_id=1, source_target_pairs={{0,31},{1,30},{2,1},{3,0},{4,3},{5,2},{6,5},{7,4},{8,7},{9,6},{10,... | collective-permute-start | bytes 393224 | tf_op jit(solution)/shard_map/ppermute | solution.py:469
  66.6 4.9 %copy-start.3 = (bf16[320,256]{1,0:T(8,128)(2,1)}, bf16[320,256]{1,0:T(8,128)(2,1)S(1)}, u32[]{:S(2)}) copy-start(bf16[320,256]{1,0:T(8,128)(2,1)S(1)} %collective-permute-done.6.high_ref) | copy-start | bytes 491524
  71.5 0.6 copy-start.6
  71.5 0.7 copy-start
  76.6 0.6 copy-start.4
  77.2 0.6 copy-start.5

commit v2 on v0

--- a/solution.py
+++ b/solution.py
@@ -1,6 +1,9 @@
+import functools
 import jax
 import jax.numpy as jnp
 from jax import lax
+from jax.experimental import pallas as pl
+from jax.experimental.pallas import tpu as pltpu
 from jax.sharding import PartitionSpec as P
 
 
@@ -109,6 +112,523 @@
     return (reduced_stiffness, reduced_mass, small_sum[None])
 
 
+BF16, F32 = jnp.bfloat16, jnp.float32
+
+
+def in_vmem(x):
+    return pltpu.with_memory_space_constraint(x, pltpu.VMEM)
+
+
+def cost(flops, moved):
+    return pl.CostEstimate(flops=int(flops), bytes_accessed=int(moved), transcendentals=0)
+
+
+def tdot(a, b):
+    return lax.dot_general(a, b, (((0,), (0,)), ((), ())), preferred_element_type=F32)
+
+
+def ndot(a, b):
+    return jnp.dot(a, b, preferred_element_type=F32)
+
+
+def rdot(a, b):
+    return lax.dot_general(a, b, (((1,), (1,)), ((), ())), preferred_element_type=F32)
+
+
+def is_even():
+    return lax.rem(lax.axis_index("sub"), 2) == lax.axis_index("col")
+
+
+def spot(map_ref, parity, cycle, sub_count):
+    found = jnp.int32(0)
+    for i in range(4):
+        label = map_ref[0, i]
+        hit = (lax.rem(label, 2) == parity) & (lax.div(label, sub_count) == cycle)
+        found += jnp.where(hit, i, 0)
+    return found
+
+
+def spots(map_ref, sub_count):
+    column = lax.axis_index("col")
+    return [
+        [spot(map_ref, parity, cycle, sub_count) for cycle in range(2)]
+        for parity in (column, 1 - column)
+    ]
+
+
+def edge_panel(row_places, column_places, edge_ref, block):
+    column = lax.axis_index("col")
+    rows = []
+    for place in row_places:
+        local = place - 2 * column
+        inside = (local >= 0) & (local < 2)
+        row = pl.multiple_of(jnp.clip(local, 0, 1) * block, block)
+        cells = []
+        for other in column_places:
+            start = pl.multiple_of(other * block, block)
+            cells.append(jnp.where(inside, edge_ref[pl.ds(row, block), pl.ds(start, block)], 0.0))
+        rows.append(jnp.concatenate(cells, axis=1))
+    return jnp.concatenate(rows, axis=0)
+
+
+def edge_diagonal(places, weight_ref, block):
+    column = lax.axis_index("col")
+    width = 2 * block
+    rows = lax.broadcasted_iota(jnp.int32, (width, width), 0)
+    columns = lax.broadcasted_iota(jnp.int32, (width, width), 1)
+    parts = []
+    for place in places:
+        local = place - 2 * column
+        inside = (local >= 0) & (local < 2)
+        parts.append(jnp.where(inside, weight_ref[pl.ds(jnp.clip(local, 0, 1), 1), :], 0.0))
+    return jnp.where(rows == columns, jnp.concatenate(parts, axis=1), 0.0)
+
+
+def scaled(mass, g):
+    half = mass.shape[1]
+    wide = g.astype(F32)
+    return jnp.concatenate([wide[:, :half] * mass, wide[:, half:] * mass], axis=1).astype(BF16)
+
+
+def halves(array):
+    upper = array.astype(BF16)
+    return upper, (array - upper.astype(F32)).astype(BF16)
+
+
+def pick_kernel(sub_count, block, map_ref, source_ref, mine_ref, head_ref, tail_ref, table_ref, stage_ref, sems):
+    depth = source_ref.shape[0]
+    head = head_ref.shape[0]
+    pieces = 2
+    rows = depth // pieces
+    lookup = pltpu.make_async_copy(map_ref, table_ref, sems.at[pieces])
+    lookup.start()
+    copies = []
+    for i in range(pieces):
+        span = pl.ds(i * rows, rows)
+        copies.append(pltpu.make_async_copy(source_ref.at[span], stage_ref.at[span], sems.at[i]))
+        copies[i].start()
+    lookup.wait()
+    mine, theirs = spots(table_ref, sub_count)
+    for i in range(pieces):
+        copies[i].wait()
+        span = pl.ds(i * rows, rows)
+        for cycle in range(2):
+            start = pl.multiple_of(mine[cycle] * block, block)
+            mine_ref[span, pl.ds(cycle * block, block)] = stage_ref[span, pl.ds(start, block)]
+    for cycle in range(2):
+        start = pl.multiple_of(theirs[cycle] * block, block)
+        lanes = pl.ds(cycle * block, block)
+        head_ref[:, lanes] = stage_ref[pl.ds(0, head), pl.ds(start, block)]
+        tail_ref[:, lanes] = stage_ref[pl.ds(head, depth - head), pl.ds(start, block)]
+
+
+def local_kernel(
+    tile,
+    a_ref,
+    mine_ref,
+    head_ref,
+    tail_ref,
+    mass_ref,
+    turned_ref,
+    before_mine_ref,
+    before_theirs_ref,
+    columns_ref,
+):
+    depth, width = mine_ref.shape
+    head = head_ref.shape[0]
+    turned_ref[pl.ds(0, width), :] = mine_ref[...].T
+    turned_ref[pl.ds(width, width), pl.ds(0, head)] = head_ref[...].T
+    turned_ref[pl.ds(width, width), pl.ds(head, depth - head)] = tail_ref[...].T
+    lanes = columns_ref.shape[1]
+    for i in range(depth // lanes):
+        line = mass_ref[:, pl.ds(i * lanes, lanes)]
+        columns_ref[pl.ds(i * lanes, lanes), :] = jnp.broadcast_to(line, (lanes, lanes)).T
+    near = pl.multiple_of(lax.axis_index("col") * depth, depth)
+    for i in range(depth // tile):
+        part = pl.ds(i * tile, tile)
+        a = a_ref[part, pl.ds(near, depth)]
+        before_mine_ref[part, :] = ndot(a, mine_ref[...])
+        before_theirs_ref[part, :] = ndot(a[:, :head], head_ref[...]) + ndot(a[:, head:], tail_ref[...])
+
+
+def middle_kernel(tile, a_ref, got_ref, before_ref, after_ref):
+    depth = before_ref.shape[0]
+    head = got_ref.shape[0]
+    far = pl.multiple_of((1 - lax.axis_index("col")) * depth, depth)
+    for i in range(depth // tile):
+        part = pl.ds(i * tile, tile)
+        after_ref[part, :] = before_ref[part, :] + ndot(a_ref[part, pl.ds(far, head)], got_ref[...])
+
+
+def first_kernel(
+    tile,
+    sub_count,
+    block,
+    map_ref,
+    a_ref,
+    got_ref,
+    before_ref,
+    columns_ref,
+    turned_ref,
+    modes_ref,
+    trial_high_ref,
+    trial_low_ref,
+    edge_ref,
+    weight_ref,
+    low_ref,
+    high_ref,
+    square_ref,
+    turned_w_ref,
+    small_ref,
+    g_ref,
+    w_ref,
+):
+    depth, width = got_ref.shape
+    even = is_even()
+    mine, theirs = spots(map_ref, sub_count)
+    far = pl.ds(pl.multiple_of((1 - lax.axis_index("col")) * depth, depth), depth)
+    for i in range(depth // tile):
+        part = pl.ds(i * tile, tile)
+        g = (-(before_ref[part, :] + ndot(a_ref[part, far], got_ref[...]))).astype(BF16)
+        w = scaled(columns_ref[part, :], g)
+        g_ref[part, :] = g
+        w_ref[part, :] = w
+    stiff = ndot(turned_ref[...], g_ref[...])
+    of_mine = (stiff[:width] + edge_panel(mine, theirs, edge_ref, block)).astype(BF16)
+    of_theirs = (stiff[width:] + edge_panel(theirs, theirs, edge_ref, block)).astype(BF16)
+    low_ref[...] = jnp.where(even, of_theirs, of_mine)
+    high_ref[...] = jnp.where(even, of_mine, of_theirs)
+    turned_w_ref[...] = w_ref[...].T
+    square = ndot(turned_w_ref[...], g_ref[...])
+    square_ref[...] = (square + edge_diagonal(theirs, weight_ref, block)).astype(BF16)
+    trial = jnp.where(even, trial_low_ref[...], trial_high_ref[...])
+    upper, lower = halves(ndot(modes_ref[...], w_ref[...]))
+    small_ref[...] = rdot(trial, upper) + rdot(trial, lower)
+
+
+def second_kernel(
+    tile,
+    a_ref,
+    got_ref,
+    before_ref,
+    columns_ref,
+    turned_w_ref,
+    square_ref,
+    modes_ref,
+    trial_high_ref,
+    trial_low_ref,
+    small_in_ref,
+    mass_low_ref,
+    mass_high_ref,
+    g_ref,
+    w_ref,
+    crossed_ref,
+    small_ref,
+):
+    depth, width = before_ref.shape
+    tail = got_ref.shape[0]
+    even = is_even()
+    far = pl.multiple_of((1 - lax.axis_index("col")) * depth + depth - tail, tail)
+    for i in range(depth // tile):
+        part = pl.ds(i * tile, tile)
+        g = (-(before_ref[part, :] + ndot(a_ref[part, pl.ds(far, tail)], got_ref[...]))).astype(BF16)
+        g_ref[part, :] = g
+        w_ref[part, :] = scaled(columns_ref[part, :], g)
+    crossed = ndot(turned_w_ref[...], g_ref[...])
+    crossed_ref[...] = crossed
+    mixed = crossed.T.astype(BF16)
+    square = square_ref[...]
+    mass_low_ref[...] = jnp.where(even, square, mixed)
+    mass_high_ref[pl.ds(0, width), :] = jnp.where(even, mixed, square)
+    trial = jnp.where(even, trial_high_ref[...], trial_low_ref[...])
+    upper, lower = halves(ndot(modes_ref[...], w_ref[...]))
+    small = small_in_ref[...] + rdot(trial, upper) + rdot(trial, lower)
+    small_ref[...] = small
+    count, modes_count = small.shape
+    mass_high_ref[pl.ds(width, count), :] = jnp.concatenate(
+        [small, jnp.zeros((count, width - modes_count), F32)], axis=1
+    ).astype(BF16)
+
+
+def third_kernel(
+    sub_count, block, map_ref, g_ref, w_ref, crossed_ref, turned_ref, edge_ref, weight_ref, back_ref, own_ref
+):
+    width = g_ref.shape[1]
+    even = is_even()
+    mine, theirs = spots(map_ref, sub_count)
+    stiff = ndot(turned_ref[...], g_ref[...])
+    of_mine = stiff[:width] + edge_panel(mine, mine, edge_ref, block)
+    of_theirs = stiff[width:] + edge_panel(theirs, mine, edge_ref, block)
+    inner = tdot(g_ref[...], w_ref[...]) + edge_diagonal(mine, weight_ref, block)
+    crossed = crossed_ref[...]
+    back_ref[0] = jnp.where(even, of_theirs, of_mine).astype(BF16)
+    back_ref[1] = jnp.where(even, crossed, inner).astype(BF16)
+    own_ref[0] = jnp.where(even, of_mine, of_theirs)
+    own_ref[1] = jnp.where(even, inner, crossed)
+
+
+def place_kernel(
+    which,
+    sub_count,
+    block,
+    own_ref,
+    high_ref,
+    back_ref,
+    cross_ref,
+    small_ref,
+    out_ref,
+    total_ref,
+    kept_ref,
+    moved_ref,
+    stage_ref,
+    sum_ref,
+    sems,
+):
+    width = 2 * block
+    copies = []
+    if which == 1:
+        count, modes_count = small_ref.shape
+        other = high_ref[pl.ds(width, count), :].astype(F32)
+        sum_ref[...] = small_ref[...] + other[:, :modes_count]
+        copies.append(pltpu.make_async_copy(sum_ref, total_ref, sems.at[4]))
+        copies[0].start()
+    half = stage_ref.shape[2] // 2
+    sub = lax.axis_index("sub")
+    even = is_even()
+    moved = back_ref[which].astype(F32) + cross_ref[...].astype(F32)
+    kept = own_ref[which] + high_ref[pl.ds(0, width), :].astype(F32)
+    kept = kept + jnp.where(even, moved, 0.0)
+    moved = jnp.where(even, 0.0, moved)
+    for k in range(2):
+        kept_ref[k] = kept[:, k * block : (k + 1) * block]
+        moved_ref[k] = moved[:, k * block : (k + 1) * block]
+    kept_spot = lax.div(jnp.where(even, sub, lax.rem(sub + sub_count - 1, sub_count)), 2)
+    moved_spot = lax.div(jnp.where(even, sub, lax.rem(sub + 1, sub_count)), 2)
+    place = lax.broadcasted_iota(jnp.int32, (half, block), 0)
+    kept_here = place == kept_spot
+    moved_here = place == moved_spot
+    group = 16
+    chunks = 2
+    rows = block // chunks
+    for p in range(2):
+        for chunk in range(chunks):
+
+            def fill(step, carry, p=p, chunk=chunk):
+                base = pl.multiple_of(step * group, group)
+                for x in range(group):
+                    row = chunk * rows + base + x
+                    parts = []
+                    for k in range(2):
+                        source = pl.ds(p * block + row, 1)
+                        a = jnp.broadcast_to(kept_ref[k, source, :], (half, block))
+                        b = jnp.broadcast_to(moved_ref[k, source, :], (half, block))
+                        parts.append(jnp.where(kept_here, a, jnp.where(moved_here, b, 0.0)))
+                    stage_ref[p, row] = jnp.concatenate(parts, axis=0).astype(BF16)
+                return carry
+
+            lax.fori_loop(0, rows // group, fill, 0)
+            span = pl.ds(chunk * rows, rows)
+            copy = pltpu.make_async_copy(
+                stage_ref.at[p, span], out_ref.at[p, span], sems.at[p * chunks + chunk]
+            )
+            copy.start()
+            copies.append(copy)
+    for copy in copies:
+        copy.wait()
+
+
+VM = pl.BlockSpec(memory_space=pltpu.VMEM)
+SM = pl.BlockSpec(memory_space=pltpu.SMEM)
+HB = pl.BlockSpec(memory_space=pltpu.HBM)
+
+
+def place(own, high, back, cross, small, which, sub_count, block, cycles):
+    width = 2 * block
+    return pl.pallas_call(
+        functools.partial(place_kernel, which, sub_count, block),
+        in_specs=[VM, VM, VM, VM, VM],
+        out_specs=[HB, HB],
+        out_shape=[
+            jax.ShapeDtypeStruct((2, block, cycles, block), BF16),
+            jax.ShapeDtypeStruct(small.shape if which == 1 else (8, block), F32),
+        ],
+        scratch_shapes=[
+            pltpu.VMEM((2, width, block), F32),
+            pltpu.VMEM((2, width, block), F32),
+            pltpu.VMEM((2, block, cycles, block), BF16),
+            pltpu.VMEM(small.shape, F32),
+            pltpu.SemaphoreType.DMA((5,)),
+        ],
+        compiler_params=pltpu.CompilerParams(vmem_limit_bytes=8 << 20),
+        cost_estimate=cost(width * cycles * block * 8, 2 * width * cycles * block),
+    )(own, in_vmem(high), in_vmem(back), in_vmem(cross), small)
+
+
+def in_hbm(x):
+    return pltpu.with_memory_space_constraint(x, pltpu.HBM)
+
+
+def pick(sub_count, block, own_map, rows, tail):
+    depth = rows.shape[0]
+    width = 2 * block
+    return pl.pallas_call(
+        functools.partial(pick_kernel, sub_count, block),
+        in_specs=[HB, HB],
+        out_specs=[VM] * 3,
+        out_shape=[
+            pltpu.VMEM((depth, width), rows.dtype),
+            pltpu.VMEM((depth - tail, width), rows.dtype),
+            pltpu.VMEM((tail, width), rows.dtype),
+        ],
+        scratch_shapes=[
+            pltpu.SMEM(own_map.shape, jnp.int32),
+            pltpu.VMEM(rows.shape, rows.dtype),
+            pltpu.SemaphoreType.DMA((3,)),
+        ],
+        compiler_params=pltpu.CompilerParams(vmem_limit_bytes=4 << 20),
+        cost_estimate=cost(depth * block, 8 * depth * block),
+        name="pick",
+    )(in_hbm(own_map), in_hbm(rows))
+
+
+def pair_shards(
+    interior_inverse,
+    interface_coupling,
+    boundary_stiffness,
+    interior_mass,
+    boundary_mass,
+    interior_modes,
+    block_map,
+    trial_vectors,
+):
+    depth = interior_inverse.shape[1]
+    block = trial_vectors.shape[2]
+    width = 2 * block
+    trials = trial_vectors.shape[0]
+    modes_count = interior_modes.shape[1]
+    sub_count = lax.axis_size("sub")
+    cycles = sub_count
+    tile = depth // 3
+    swap = [(0, 1), (1, 0)]
+    both = ("sub", "col")
+    back_route = [(i, (i - 1) % sub_count) for i in range(sub_count)]
+    cross_route = [
+        (2 * i + c, 2 * ((i - 1) % sub_count) + 1 - c) for i in range(sub_count) for c in range(2)
+    ]
+    params = pltpu.CompilerParams(vmem_limit_bytes=12 << 20)
+    mine, head, tail = pick(sub_count, block, block_map, interface_coupling[0], depth // 4)
+    got_theirs = in_vmem(lax.ppermute(mine, "col", swap))
+    got_head = in_vmem(lax.ppermute(head, "col", swap))
+    got_tail = in_vmem(lax.ppermute(tail, "col", swap))
+    previous_trial = shifted(trial_vectors, "sub", 1)
+    trial_high = in_vmem(trial_vectors.reshape(trials, width))
+    trial_low = in_vmem(previous_trial.reshape(trials, width))
+    inverse_rows = in_vmem(interior_inverse[0])
+    edge = in_vmem(boundary_stiffness[0])
+    modes = in_vmem(interior_modes[0])
+    weights = in_vmem(boundary_mass[0].reshape(2, block))
+
+    turned, before_mine, before_theirs, columns = pl.pallas_call(
+        functools.partial(local_kernel, tile),
+        in_specs=[VM] * 5,
+        out_specs=[VM] * 4,
+        out_shape=[
+            pltpu.VMEM((2 * width, depth), BF16),
+            pltpu.VMEM((depth, width), F32),
+            pltpu.VMEM((depth, width), F32),
+            pltpu.VMEM((depth, block), F32),
+        ],
+        compiler_params=params,
+        cost_estimate=cost(4 * depth * depth * width, 2 * depth * depth),
+        name="local",
+    )(inverse_rows, mine, head, tail, in_vmem(interior_mass))
+    stiff_low, stiff_high, square, turned_w, small_first = pl.pallas_call(
+        functools.partial(first_kernel, tile, sub_count, block),
+        in_specs=[SM] + [VM] * 10,
+        out_specs=[VM] * 5,
+        out_shape=[
+            pltpu.VMEM((width, width), BF16),
+            pltpu.VMEM((width, width), BF16),
+            pltpu.VMEM((width, width), BF16),
+            pltpu.VMEM((width, depth), BF16),
+            pltpu.VMEM((trials, modes_count), F32),
+        ],
+        scratch_shapes=[pltpu.VMEM((depth, width), BF16), pltpu.VMEM((depth, width), BF16)],
+        compiler_params=params,
+        cost_estimate=cost(4 * depth * depth * width, 2 * depth * depth),
+        name="first",
+    )(
+        block_map,
+        inverse_rows,
+        got_theirs,
+        before_theirs,
+        columns,
+        turned,
+        modes,
+        trial_high,
+        trial_low,
+        edge,
+        weights,
+    )
+    cross_stiff = lax.ppermute(stiff_low, both, cross_route)
+    high_stiff = lax.ppermute(stiff_high, "col", swap)
+    after_mine = pl.pallas_call(
+        functools.partial(middle_kernel, tile),
+        in_specs=[VM] * 3,
+        out_specs=VM,
+        out_shape=pltpu.VMEM((depth, width), F32),
+        compiler_params=params,
+        cost_estimate=cost(2 * depth * depth * width, 2 * depth * depth),
+        name="middle",
+    )(inverse_rows, got_head, before_mine)
+    mass_low, mass_high, g_mine, w_mine, crossed, small = pl.pallas_call(
+        functools.partial(second_kernel, tile),
+        in_specs=[VM] * 10,
+        out_specs=[VM] * 6,
+        out_shape=[
+            pltpu.VMEM((width, width), BF16),
+            pltpu.VMEM((width + trials, width), BF16),
+            pltpu.VMEM((depth, width), BF16),
+            pltpu.VMEM((depth, width), BF16),
+            pltpu.VMEM((width, width), F32),
+            pltpu.VMEM((trials, modes_count), F32),
+        ],
+        compiler_params=params,
+        cost_estimate=cost(2 * depth * depth * width, 2 * depth * depth),
+        name="second",
+    )(
+        inverse_rows,
+        got_tail,
+        after_mine,
+        columns,
+        turned_w,
+        square,
+        modes,
+        trial_high,
+        trial_low,
+        small_first,
+    )
+    back, own = pl.pallas_call(
+        functools.partial(third_kernel, sub_count, block),
+        in_specs=[SM] + [VM] * 6,
+        out_specs=[VM] * 2,
+        out_shape=[pltpu.VMEM((2, width, width), BF16), pltpu.VMEM((2, width, width), F32)],
+        compiler_params=params,
+        cost_estimate=cost(8 * depth * width * width, 10 * depth * width),
+        name="third",
+    )(block_map, g_mine, w_mine, crossed, turned, edge, weights)
+    back_here = lax.ppermute(back, "sub", back_route)
+    cross_mass = lax.ppermute(mass_low, both, cross_route)
+    high_mass = lax.ppermute(mass_high, "col", swap)
+    reduced_stiffness, _ = place(
+        own, high_stiff, back_here, cross_stiff, small, 0, sub_count, block, cycles
+    )
+    reduced_mass, summed = place(
+        own, high_mass, back_here, cross_mass, small, 1, sub_count, block, cycles
+    )
+    return (reduced_stiffness, reduced_mass, summed[None])
+
+
 def solution(mesh):
     placed = (
         P("sub", "col", None),
@@ -120,8 +640,9 @@
         P("sub", None),
         P(None, None, "sub"),
     )
+    paired = mesh.shape["col"] == 2 and mesh.shape["sub"] % 2 == 0
     return jax.shard_map(
-        shards,
+        pair_shards if paired else shards,
         mesh=mesh,
         in_specs=placed,
         out_specs=(P(None, "sub", None, "col"), P(None, "sub", None, "col"), P("sub", None, None)),

time: 170 us -> 61 us (0.36)
  waiting for transfers between devices: 102 us -> 29.5 us
  matrix products: 27.1 us -> 0 us
  Pallas kernels: 0 us -> 13.6 us
  between operations: 14.3 us -> 0.79 us
  blocking collectives: 10.1 us -> 0 us
  starting transfers between devices: 8 us -> 13.2 us
  local copies, waits for them, and re-layouts: 7.84 us -> 3.72 us
    all_gather x1 -> x0, waiting for transfers between devices: 47.1 us -> none  [shards(): lax.all_gather(coupling_rows, 'col', axis=0, tiled=True)]
    psum x1 -> x0, waiting for transfers between devices: 43.1 us -> none  [shards(): lax.psum((stiff_part, mass_part, small_part), 'col')]
    ppermute x0 -> x8, waiting for transfers between devices: none -> 29.5 us  [the longest x1 22.5 us: pair_shards(): got_head = in_vmem(lax.ppermute(head, 'col', swap))]
    dot_general x14 -> x0, matrix products: 27.1 us -> none  [the longest x1 9.45 us: shards(): jnp.dot(inverse_rows, lax.all_gather(coupling_rows, 'col', axis=0, tiled=...]
    pallas_call x0 -> x8, Pallas kernels: none -> 13.6 us  [the longest x1 2.97 us: pair_shards(): pl.pallas_call(functools.partial(first_kernel, tile, sub_count, block), i...]
    ppermute x0 -> x8, starting transfers between devices: none -> 13.2 us  [the longest x1 3.03 us: pair_shards(): got_theirs = in_vmem(lax.ppermute(mine, 'col', swap))]
    ppermute x4 -> x1, waiting for transfers between devices: 10.9 us -> 0.01 us  [shifted(): return lax.ppermute(block, axis, route)]
    psum x1 -> x0, blocking collectives: 10.1 us -> none  [shards(): lax.psum((stiff_part, mass_part, small_part), 'col')]
  transfers between devices with their start and end apart: 6 -> 9, of which waited for: 5 -> 4; matrix products, arithmetic and copies ran while one was open for 10% -> 0% of each run, Pallas kernels for 0% -> 13%
where the time goes in v2:
time: 61 us; the launch traced here: 60.8 us
  waiting for transfers between devices  29.5 us (48%)
  Pallas kernels  13.6 us (22%)
  starting transfers between devices  13.2 us (22%)
  local copies, waits for them, and re-layouts  3.72 us (6%)
  between operations  0.79 us (1%)
    ppermute x1, waiting for transfers between devices, pair_shards(): got_head = in_vmem(lax.ppermute(head, 'col', swap))  22.5 us
    ppermute x1, waiting for transfers between devices, pair_shards(): cross_mass = lax.ppermute(mass_low, both, cross_route)  4.43 us
    unnamed x18, local copies, waits for them, and re-layouts  3.72 us
    ppermute x1, starting transfers between devices, pair_shards(): got_theirs = in_vmem(lax.ppermute(mine, 'col', swap))  3.03 us
    pallas_call x1, Pallas kernels, pair_shards(): pl.pallas_call(functools.partial(first_kernel, tile, sub_count, block), i...  2.97 us
    pallas_call x1, Pallas kernels, pair_shards(): pl.pallas_call(functools.partial(local_kernel, tile), in_specs=[VM] * 5,...  2.81 us
    ppermute x1, starting transfers between devices, pair_shards(): back_here = lax.ppermute(back, 'sub', back_route)  2.6 us
    ppermute x1, starting transfers between devices, pair_shards(): cross_mass = lax.ppermute(mass_low, both, cross_route)  2.46 us
  transfers between devices with their start and end apart: 9, of which 4 were waited for; matrix products, arithmetic and copies ran while one was open for 0% of the time, Pallas kernels for 13%

profile of v2, /device:TPU:0, one launch (start us, length us, event | category | flops | bytes accessed | tf_op | source)
XLA Modules:
  0.0 60.8 jit_solution(583090517440491213)
XLA Ops:
  0.6 0.0 copy-start.7
  0.6 0.0 copy-start.4
  0.7 1.6 %pick.1 = (bf16[1536,256]{1,0:T(8,128)(2,1)S(1)}, bf16[1152,256]{1,0:T(8,128)(2,1)S(1)}, bf16[384,256]{1,0:T(8,128)(2,1)S(1)}) custom-call(s32[1,4]{1,0:T(1,128)} %map_ref.5, bf16[1536,512]{1,0:T(8,128)(2,1)} %bitcast.28), custom_call_target="tpu_custom_call" | custom-call | flops 196608 | bytes 1572864 | tf_op jit(solution)/shard_map/pick/pallas_call | solution.py:474
  2.3 3.0 %collective-permute-start.2 = (bf16[1536,256]{1,0:T(8,128)(2,1)S(1)}, bf16[1536,256]{1,0:T(8,128)(2,1)S(1)}, u32[]{:S(2)}, u32[]{:S(2)}) collective-permute-start(bf16[1536,256]{1,0:T(8,128)(2,1)S(1)} %get-tuple-element.28.mine_ref), channel_id=1, source_target_pairs={{0,1},{1,0},{2,3},{3,2},{4,5},{5,4},{6,7},{7,6},{8,9},{9,8},{10,11... | collective-permute-start | bytes 2359304 | tf_op jit(solution)/shard_map/ppermute | solution.py:520
  5.3 0.1 collective-permute-start.1
  5.4 0.0 collective-permute-start.3
  5.4 1.9 %collective-permute-start = (bf16[384,256]{1,0:T(8,128)(2,1)S(1)}, bf16[384,256]{1,0:T(8,128)(2,1)S(1)}, u32[]{:S(2)}, u32[]{:S(2)}) collective-permute-start(bf16[384,256]{1,0:T(8,128)(2,1)S(1)} %get-tuple-element.26.tail_ref), channel_id=1, source_target_pairs={{0,1},{1,0},{2,3},{3,2},{4,5},{5,4},{6,7},{7,6},{8,9},{9,8},{10,11... | collective-permute-start | bytes 589832 | tf_op jit(solution)/shard_map/ppermute | solution.py:522
  7.3 0.0 copy-done.4
  7.3 3.7 %copy-done = bf16[1,1536,3072]{2,1,0:T(8,128)(2,1)S(1)} copy-done((bf16[1,1536,3072]{2,1,0:T(8,128)(2,1)S(1)}, bf16[1,1536,3072]{2,1,0:T(8,128)(2,1)}, u32[]{:S(2)}) %copy-start) | copy-done | bytes 9437208
  11.0 2.8 %local.1 = (bf16[512,1536]{1,0:T(8,128)(2,1)S(1)}, f32[1536,256]{1,0:T(8,128)S(1)}, f32[1536,256]{1,0:T(8,128)S(1)}, f32[1536,128]{1,0:T(8,128)S(1)}) custom-call(bf16[1536,3072]{1,0:T(8,128)(2,1)S(1)} %bitcast.14, bf16[1536,256]{1,0:T(8,128)(2,1)S(1)} %get-tuple-element.28.mine_ref, bf16[1152,256]{1,0:T(8,128)(2,1)S(1)} %get-tuple-element.27.head_ref, ...), custom_call_target="tpu_custom_call" | custom-call | flops 2415919104 | bytes 4718592 | tf_op jit(solution)/shard_map/local/pallas_call | solution.py:531
  13.8 0.0 collective-permute-done.3
  13.9 22.5 %collective-permute-done.1.got_ref = bf16[1152,256]{1,0:T(8,128)(2,1)S(1)} collective-permute-done((bf16[1152,256]{1,0:T(8,128)(2,1)S(1)}, bf16[1152,256]{1,0:T(8,128)(2,1)S(1)}, u32[]{:S(2)}, u32[]{:S(2)}) %collective-permute-start.1) | collective-permute-done | bytes 589856 | tf_op jit(solution)/shard_map/ppermute | solution.py:521
  36.3 0.0 copy-done.1
  36.3 0.0 copy-start.6
  36.4 1.2 %middle.1.before_ref = f32[1536,256]{1,0:T(8,128)S(1)} custom-call(bf16[1536,3072]{1,0:T(8,128)(2,1)S(1)} %bitcast.15, bf16[1152,256]{1,0:T(8,128)(2,1)S(1)} %collective-permute-done.1.got_ref, f32[1536,256]{1,0:T(8,128)S(1)} %get-tuple-element.29.before_ref), custom_call_target="tpu_custom_call" | custom-call | flops 1207959552 | bytes 4718592 | tf_op jit(solution)/shard_map/middle/pallas_call | solution.py:575
  37.6 0.0 collective-permute-done.2.got_ref
  37.6 3.0 %first.1 = (bf16[256,256]{1,0:T(8,128)(2,1)S(1)}, bf16[256,256]{1,0:T(8,128)(2,1)S(1)}, bf16[256,256]{1,0:T(8,128)(2,1)S(1)}, bf16[256,1536]{1,0:T(8,128)(2,1)S(1)}, f32[64,200]{1,0:T(8,128)S(1)}) custom-call(s32[1,4]{1,0:T(1,128)S(1)} %copy-done.5, bf16[1536,3072]{1,0:T(8,128)(2,1)S(1)} %bitcast.16, bf16[1536,256]{1,0:T(8,128)(2,1)S(1)} %collective-permute-done.2.got_ref, ...), custom_call_target="tpu_custom_call" | custom-call | flops 2415919104 | bytes 4718592 | tf_op jit(solution)/shard_map/first/pallas_call | solution.py:545
  40.6 0.0 collective-permute-done.got_ref
  40.6 1.2 %second.1 = (bf16[256,256]{1,0:T(8,128)(2,1)S(1)}, bf16[320,256]{1,0:T(8,128)(2,1)S(1)}, bf16[1536,256]{1,0:T(8,128)(2,1)S(1)}, bf16[1536,256]{1,0:T(8,128)(2,1)...) custom-call(bf16[1536,3072]{1,0:T(8,128)(2,1)S(1)} %bitcast.17, bf16[384,256]{1,0:T(8,128)(2,1)S(1)} %collective-permute-done.got_ref, ...), custom_call_target="tpu_custom_call" | custom-call | flops 1207959552 | bytes 4718592 | tf_op jit(solution)/shard_map/second/pallas_call | solution.py:584
  41.9 1.4 %third.1 = (bf16[2,256,256]{2,1,0:T(8,128)(2,1)S(1)}, f32[2,256,256]{2,1,0:T(8,128)S(1)}) custom-call(s32[1,4]{1,0:T(1,128)S(1)} %copy-done.5, bf16[1536,256]{1,0:T(8,128)(2,1)S(1)} %get-tuple-element.36.g_ref, bf16[1536,256]{1,0:T(8,128)(2,1)S(1)} %get-tuple-element.37.w_ref, f32[256,256]{1,0:T(8,128)S(1)} %get-tuple-element.38.crossed_ref, ...), custom_call_target="tpu_custom_call" | custom-call | flops 805306368 | bytes 3932160 | tf_op jit(solution)/shard_map/third/pallas_call | solution.py:611
  43.3 2.6 %collective-permute-start.5 = (bf16[2,256,256]{2,1,0:T(8,128)(2,1)S(1)}, bf16[2,256,256]{2,1,0:T(8,128)(2,1)S(1)}, u32[]{:S(2)}, u32[]{:S(2)}) collective-permute-start(bf16[2,256,256]{2,1,0:T(8,128)(2,1)S(1)} %get-tuple-element.41), channel_id=1, source_target_pairs={{0,30},{2,0},{4,2},{6,4},{8,6},{10,8},{12,10},{14,12},{16,14},{18,... | collective-permute-start | bytes 786440 | tf_op jit(solution)/shard_map/ppermute | solution.py:620
  45.9 1.4 %collective-permute-start.7 = (bf16[320,256]{1,0:T(8,128)(2,1)S(1)}, bf16[320,256]{1,0:T(8,128)(2,1)S(1)}, u32[]{:S(2)}, u32[]{:S(2)}) collective-permute-start(bf16[320,256]{1,0:T(8,128)(2,1)S(1)} %get-tuple-element.45), channel_id=1, source_target_pairs={{0,1},{1,0},{2,3},{3,2},{4,5},{5,4},{6,7},{7,6},{8,9},{9,8},{10,11... | collective-permute-start | bytes 491528 | tf_op jit(solution)/shard_map/ppermute | solution.py:622
  47.2 2.5 %collective-permute-start.8 = (bf16[256,256]{1,0:T(8,128)(2,1)S(1)}, bf16[256,256]{1,0:T(8,128)(2,1)S(1)}, u32[]{:S(2)}, u32[]{:S(2)}) collective-permute-start(bf16[256,256]{1,0:T(8,128)(2,1)S(1)} %get-tuple-element.46), channel_id=1, source_target_pairs={{0,31},{1,30},{2,1},{3,0},{4,3},{5,2},{6,5},{7,4},{8,7},{9,6},{10,... | collective-permute-start | bytes 393224 | tf_op jit(solution)/shard_map/ppermute | solution.py:621
  49.7 1.4 %collective-permute-start.4 = (bf16[256,256]{1,0:T(8,128)(2,1)S(1)}, bf16[256,256]{1,0:T(8,128)(2,1)S(1)}, u32[]{:S(2)}, u32[]{:S(2)}) collective-permute-start(bf16[256,256]{1,0:T(8,128)(2,1)S(1)} %get-tuple-element.40), channel_id=1, source_target_pairs={{0,1},{1,0},{2,3},{3,2},{4,5},{5,4},{6,7},{7,6},{8,9},{9,8},{10,11... | collective-permute-start | bytes 393224 | tf_op jit(solution)/shard_map/ppermute | solution.py:574
  51.1 0.3 collective-permute-start.6
  51.4 4.4 %collective-permute-done.8.cross_ref = bf16[256,256]{1,0:T(8,128)(2,1)S(1)} collective-permute-done((bf16[256,256]{1,0:T(8,128)(2,1)S(1)}, bf16[256,256]{1,0:T(8,128)(2,1)S(1)}, u32[]{:S(2)}, u32[]{:S(2)}) %collective-permute-start.8) | collective-permute-done | bytes 131104 | tf_op jit(solution)/shard_map/ppermute | solution.py:621
  55.9 0.0 collective-permute-done.7.high_ref
  55.9 0.0 collective-permute-done.5.back_ref
  55.9 1.2 %shard_map.104 = (bf16[2,128,16,128]{3,2,1,0:T(8,128)(2,1)}, f32[64,200]{1,0:T(8,128)}) custom-call(f32[2,256,256]{2,1,0:T(8,128)S(1)} %get-tuple-element.39.own_ref, bf16[320,256]{1,0:T(8,128)(2,1)S(1)} %collective-permute-done.7.high_ref, bf16[2,256,256]{2,1,0:T(8,128)(2,1)S(1)} %collective-permute-done.5.back_ref, ...), custom_call_target="tpu_custom_call" | custom-call | flops 4194304 | bytes 1048576 | tf_op jit(solution)/shard_map/pallas_call | solution.py:447
  57.0 0.7 %collective-permute-done.4.high_ref = bf16[256,256]{1,0:T(8,128)(2,1)S(1)} collective-permute-done((bf16[256,256]{1,0:T(8,128)(2,1)S(1)}, bf16[256,256]{1,0:T(8,128)(2,1)S(1)}, u32[]{:S(2)}, u32[]{:S(2)}) %collective-permute-start.4) | collective-permute-done | bytes 131104 | tf_op jit(solution)/shard_map/ppermute | solution.py:574
  57.7 1.9 %collective-permute-done.6.cross_ref = bf16[256,256]{1,0:T(8,128)(2,1)S(1)} collective-permute-done((bf16[256,256]{1,0:T(8,128)(2,1)S(1)}, bf16[256,256]{1,0:T(8,128)(2,1)S(1)}, u32[]{:S(2)}, u32[]{:S(2)}) %collective-permute-start.6) | collective-permute-done | bytes 131104 | tf_op jit(solution)/shard_map/ppermute | solution.py:573
  59.6 1.2 %shard_map.103 = (bf16[2,128,16,128]{3,2,1,0:T(8,128)(2,1)}, f32[8,128]{1,0:T(8,128)}) custom-call(f32[2,256,256]{2,1,0:T(8,128)S(1)} %get-tuple-element.39.own_ref, bf16[256,256]{1,0:T(8,128)(2,1)S(1)} %collective-permute-done.4.high_ref, bf16[2,256,256]{2,1,0:T(8,128)(2,1)S(1)} %collective-permute-done.5.back_ref, ...), custom_call_target="tpu_custom_call" | custom-call | flops 4194304 | bytes 1048576 | tf_op jit(solution)/shard_map/pallas_call | solution.py:447
  (12 shorter events, 0.0 us)
Async XLA Ops:
  0.6 4.8 %copy-start.7 = (bf16[64,2,128]{2,1,0:T(2,128)(2,1)S(1)}, bf16[64,2,128]{2,1,0:T(2,128)(2,1)}, u32[]{:S(2)}) copy-start(bf16[64,2,128]{2,1,0:T(2,128)(2,1)} %param.15) | copy-start | bytes 98308
  0.6 6.7 %copy-start.4 = (f32[1,1536]{1,0:T(1,128)S(1)}, f32[1,1536]{1,0:T(1,128)}, u32[]{:S(2)}) copy-start(f32[1,1536]{1,0:T(1,128)} %mass_ref.1) | copy-start | bytes 18436
  2.3 35.3 %collective-permute-start.2 = (bf16[1536,256]{1,0:T(8,128)(2,1)S(1)}, bf16[1536,256]{1,0:T(8,128)(2,1)S(1)}, u32[]{:S(2)}, u32[]{:S(2)}) collective-permute-start(bf16[1536,256]{1,0:T(8,128)(2,1)S(1)} %get-tuple-element.28.mine_ref), channel_id=1, source_target_pairs={{0,1},{1,0},{2,3},{3,2},{4,5},{5,4},{6,7},{7,6},{8,9},{9,8},{10,11... | collective-permute-start | bytes 2359304 | tf_op jit(solution)/shard_map/ppermute | solution.py:520
  5.3 31.0 %collective-permute-start.1 = (bf16[1152,256]{1,0:T(8,128)(2,1)S(1)}, bf16[1152,256]{1,0:T(8,128)(2,1)S(1)}, u32[]{:S(2)}, u32[]{:S(2)}) collective-permute-start(bf16[1152,256]{1,0:T(8,128)(2,1)S(1)} %get-tuple-element.27.head_ref), channel_id=1, source_target_pairs={{0,1},{1,0},{2,3},{3,2},{4,5},{5,4},{6,7},{7,6},{8,9},{9,8},{10,11... | collective-permute-start | bytes 1769480 | tf_op jit(solution)/shard_map/ppermute | solution.py:521
  5.4 8.5 %collective-permute-start.3 = (bf16[64,2,128]{2,1,0:T(2,128)(2,1)S(1)}, bf16[64,2,128]{2,1,0:T(2,128)(2,1)S(1)}, u32[]{:S(2)}, u32[]{:S(2)}) collective-permute-start(bf16[64,2,128]{2,1,0:T(2,128)(2,1)S(1)} %copy-done.7), channel_id=1, source_target_pairs={{30,0},{0,2},{2,4},{4,6},{6,8},{8,10},{10,12},{12,14},{14,16},{16,... | collective-permute-start | bytes 98312 | tf_op jit(solution)/shard_map/ppermute | solution.py:13
  5.4 35.2 %collective-permute-start = (bf16[384,256]{1,0:T(8,128)(2,1)S(1)}, bf16[384,256]{1,0:T(8,128)(2,1)S(1)}, u32[]{:S(2)}, u32[]{:S(2)}) collective-permute-start(bf16[384,256]{1,0:T(8,128)(2,1)S(1)} %get-tuple-element.26.tail_ref), channel_id=1, source_target_pairs={{0,1},{1,0},{2,3},{3,2},{4,5},{5,4},{6,7},{7,6},{8,9},{9,8},{10,11... | collective-permute-start | bytes 589832 | tf_op jit(solution)/shard_map/ppermute | solution.py:522
  7.3 3.7 %copy-start = (bf16[1,1536,3072]{2,1,0:T(8,128)(2,1)S(1)}, bf16[1,1536,3072]{2,1,0:T(8,128)(2,1)}, u32[]{:S(2)}) copy-start(bf16[1,1536,3072]{2,1,0:T(8,128)(2,1)} %param.8) | copy-start | bytes 28311556
  11.0 25.3 %copy-start.1 = (bf16[1,1536,3072]{2,1,0:T(8,128)(2,1)S(1)}, bf16[1,1536,3072]{2,1,0:T(8,128)(2,1)}, u32[]{:S(2)}) copy-start(bf16[1,1536,3072]{2,1,0:T(8,128)(2,1)} %param.8) | copy-start | bytes 28311556
  36.3 1.3 %copy-start.2 = (bf16[1,200,1536]{2,1,0:T(8,128)(2,1)S(1)}, bf16[1,200,1536]{2,1,0:T(8,128)(2,1)}, u32[]{:S(2)}) copy-start(bf16[1,200,1536]{2,1,0:T(8,128)(2,1)} %param.13) | copy-start | bytes 1843204
  36.3 1.3 %copy-start.3 = (f32[1,256,512]{2,1,0:T(8,128)S(1)}, f32[1,256,512]{2,1,0:T(8,128)}, u32[]{:S(2)}) copy-start(f32[1,256,512]{2,1,0:T(8,128)} %param.10) | copy-start | bytes 1572868
  36.3 1.3 %copy-start.5 = (s32[1,4]{1,0:T(1,128)S(1)}, s32[1,4]{1,0:T(1,128)}, u32[]{:S(2)}) copy-start(s32[1,4]{1,0:T(1,128)} %map_ref.5) | copy-start | bytes 52
  36.3 1.3 %copy-start.6 = (f32[1,256]{1,0:T(1,128)S(1)}, f32[1,256]{1,0:T(1,128)}, u32[]{:S(2)}) copy-start(f32[1,256]{1,0:T(1,128)} %param.12) | copy-start | bytes 3076
  43.3 12.6 %collective-permute-start.5 = (bf16[2,256,256]{2,1,0:T(8,128)(2,1)S(1)}, bf16[2,256,256]{2,1,0:T(8,128)(2,1)S(1)}, u32[]{:S(2)}, u32[]{:S(2)}) collective-permute-start(bf16[2,256,256]{2,1,0:T(8,128)(2,1)S(1)} %get-tuple-element.41), channel_id=1, source_target_pairs={{0,30},{2,0},{4,2},{6,4},{8,6},{10,8},{12,10},{14,12},{16,14},{18,... | collective-permute-start | bytes 786440 | tf_op jit(solution)/shard_map/ppermute | solution.py:620
  45.9 10.0 %collective-permute-start.7 = (bf16[320,256]{1,0:T(8,128)(2,1)S(1)}, bf16[320,256]{1,0:T(8,128)(2,1)S(1)}, u32[]{:S(2)}, u32[]{:S(2)}) collective-permute-start(bf16[320,256]{1,0:T(8,128)(2,1)S(1)} %get-tuple-element.45), channel_id=1, source_target_pairs={{0,1},{1,0},{2,3},{3,2},{4,5},{5,4},{6,7},{7,6},{8,9},{9,8},{10,11... | collective-permute-start | bytes 491528 | tf_op jit(solution)/shard_map/ppermute | solution.py:622
  47.2 8.6 %collective-permute-start.8 = (bf16[256,256]{1,0:T(8,128)(2,1)S(1)}, bf16[256,256]{1,0:T(8,128)(2,1)S(1)}, u32[]{:S(2)}, u32[]{:S(2)}) collective-permute-start(bf16[256,256]{1,0:T(8,128)(2,1)S(1)} %get-tuple-element.46), channel_id=1, source_target_pairs={{0,31},{1,30},{2,1},{3,0},{4,3},{5,2},{6,5},{7,4},{8,7},{9,6},{10,... | collective-permute-start | bytes 393224 | tf_op jit(solution)/shard_map/ppermute | solution.py:621
  49.7 8.0 %collective-permute-start.4 = (bf16[256,256]{1,0:T(8,128)(2,1)S(1)}, bf16[256,256]{1,0:T(8,128)(2,1)S(1)}, u32[]{:S(2)}, u32[]{:S(2)}) collective-permute-start(bf16[256,256]{1,0:T(8,128)(2,1)S(1)} %get-tuple-element.40), channel_id=1, source_target_pairs={{0,1},{1,0},{2,3},{3,2},{4,5},{5,4},{6,7},{7,6},{8,9},{9,8},{10,11... | collective-permute-start | bytes 393224 | tf_op jit(solution)/shard_map/ppermute | solution.py:574
  51.1 8.5 %collective-permute-start.6 = (bf16[256,256]{1,0:T(8,128)(2,1)S(1)}, bf16[256,256]{1,0:T(8,128)(2,1)S(1)}, u32[]{:S(2)}, u32[]{:S(2)}) collective-permute-start(bf16[256,256]{1,0:T(8,128)(2,1)S(1)} %get-tuple-element.42), channel_id=1, source_target_pairs={{0,31},{1,30},{2,1},{3,0},{4,3},{5,2},{6,5},{7,4},{8,7},{9,6},{10,... | collective-permute-start | bytes 393224 | tf_op jit(solution)/shard_map/ppermute | solution.py:573

commit v3 on v2

--- a/solution.py
+++ b/solution.py
@@ -136,14 +136,14 @@
 
 
 def is_even():
-    return lax.rem(lax.axis_index("sub"), 2) == lax.axis_index("col")
+    return (lax.axis_index("sub") & 1) == lax.axis_index("col")
 
 
 def spot(map_ref, parity, cycle, sub_count):
     found = jnp.int32(0)
     for i in range(4):
         label = map_ref[0, i]
-        hit = (lax.rem(label, 2) == parity) & (lax.div(label, sub_count) == cycle)
+        hit = ((label & 1) == parity) & ((label >= sub_count) == (cycle == 1))
         found += jnp.where(hit, i, 0)
     return found
 
@@ -195,9 +195,25 @@
     return upper, (array - upper.astype(F32)).astype(BF16)
 
 
-def pick_kernel(sub_count, block, map_ref, source_ref, mine_ref, head_ref, tail_ref, table_ref, stage_ref, sems):
+def lead_kernel(sub_count, block, map_ref, source_ref, lead_ref, table_ref, stage_ref, sems):
+    lookup = pltpu.make_async_copy(map_ref, table_ref, sems.at[0])
+    lookup.start()
+    copy = pltpu.make_async_copy(source_ref.at[pl.ds(0, lead_ref.shape[0])], stage_ref, sems.at[1])
+    copy.start()
+    lookup.wait()
+    mine, _ = spots(table_ref, sub_count)
+    copy.wait()
+    for cycle in range(2):
+        start = pl.multiple_of(mine[cycle] * block, block)
+        lead_ref[:, pl.ds(cycle * block, block)] = stage_ref[:, pl.ds(start, block)]
+
+
+def pick_kernel(
+    sub_count, block, map_ref, source_ref, rest_ref, head_ref, tail_ref, table_ref, stage_ref, sems
+):
     depth = source_ref.shape[0]
     head = head_ref.shape[0]
+    lead = depth - rest_ref.shape[0]
     pieces = 2
     rows = depth // pieces
     lookup = pltpu.make_async_copy(map_ref, table_ref, sems.at[pieces])
@@ -209,12 +225,12 @@
         copies[i].start()
     lookup.wait()
     mine, theirs = spots(table_ref, sub_count)
-    for i in range(pieces):
-        copies[i].wait()
-        span = pl.ds(i * rows, rows)
-        for cycle in range(2):
-            start = pl.multiple_of(mine[cycle] * block, block)
-            mine_ref[span, pl.ds(cycle * block, block)] = stage_ref[span, pl.ds(start, block)]
+    for copy in copies:
+        copy.wait()
+    for cycle in range(2):
+        start = pl.multiple_of(mine[cycle] * block, block)
+        lanes = pl.ds(cycle * block, block)
+        rest_ref[:, lanes] = stage_ref[pl.ds(lead, depth - lead), pl.ds(start, block)]
     for cycle in range(2):
         start = pl.multiple_of(theirs[cycle] * block, block)
         lanes = pl.ds(cycle * block, block)
@@ -225,7 +241,8 @@
 def local_kernel(
     tile,
     a_ref,
-    mine_ref,
+    lead_ref,
+    rest_ref,
     head_ref,
     tail_ref,
     mass_ref,
@@ -234,9 +251,11 @@
     before_theirs_ref,
     columns_ref,
 ):
-    depth, width = mine_ref.shape
+    depth, width = before_mine_ref.shape
+    lead = lead_ref.shape[0]
     head = head_ref.shape[0]
-    turned_ref[pl.ds(0, width), :] = mine_ref[...].T
+    turned_ref[pl.ds(0, width), pl.ds(0, lead)] = lead_ref[...].T
+    turned_ref[pl.ds(0, width), pl.ds(lead, depth - lead)] = rest_ref[...].T
     turned_ref[pl.ds(width, width), pl.ds(0, head)] = head_ref[...].T
     turned_ref[pl.ds(width, width), pl.ds(head, depth - head)] = tail_ref[...].T
     lanes = columns_ref.shape[1]
@@ -247,7 +266,7 @@
     for i in range(depth // tile):
         part = pl.ds(i * tile, tile)
         a = a_ref[part, pl.ds(near, depth)]
-        before_mine_ref[part, :] = ndot(a, mine_ref[...])
+        before_mine_ref[part, :] = ndot(a[:, :lead], lead_ref[...]) + ndot(a[:, lead:], rest_ref[...])
         before_theirs_ref[part, :] = ndot(a[:, :head], head_ref[...]) + ndot(a[:, head:], tail_ref[...])
 
 
@@ -266,7 +285,8 @@
     block,
     map_ref,
     a_ref,
-    got_ref,
+    lead_ref,
+    rest_ref,
     before_ref,
     columns_ref,
     turned_ref,
@@ -283,13 +303,16 @@
     g_ref,
     w_ref,
 ):
-    depth, width = got_ref.shape
+    depth, width = before_ref.shape
+    lead = lead_ref.shape[0]
     even = is_even()
     mine, theirs = spots(map_ref, sub_count)
-    far = pl.ds(pl.multiple_of((1 - lax.axis_index("col")) * depth, depth), depth)
+    far = pl.multiple_of((1 - lax.axis_index("col")) * depth, depth)
     for i in range(depth // tile):
         part = pl.ds(i * tile, tile)
-        g = (-(before_ref[part, :] + ndot(a_ref[part, far], got_ref[...]))).astype(BF16)
+        a = a_ref[part, pl.ds(far, depth)]
+        total = before_ref[part, :] + ndot(a[:, :lead], lead_ref[...]) + ndot(a[:, lead:], rest_ref[...])
+        g = (-total).astype(BF16)
         w = scaled(columns_ref[part, :], g)
         g_ref[part, :] = g
         w_ref[part, :] = w
@@ -402,8 +425,10 @@
     for k in range(2):
         kept_ref[k] = kept[:, k * block : (k + 1) * block]
         moved_ref[k] = moved[:, k * block : (k + 1) * block]
-    kept_spot = lax.div(jnp.where(even, sub, lax.rem(sub + sub_count - 1, sub_count)), 2)
-    moved_spot = lax.div(jnp.where(even, sub, lax.rem(sub + 1, sub_count)), 2)
+    before = jnp.where(sub == 0, sub_count - 1, sub - 1)
+    after = jnp.where(sub == sub_count - 1, 0, sub + 1)
+    kept_spot = jnp.where(even, sub, before) >> 1
+    moved_spot = jnp.where(even, sub, after) >> 1
     place = lax.broadcasted_iota(jnp.int32, (half, block), 0)
     kept_here = place == kept_spot
     moved_here = place == moved_spot
@@ -468,7 +493,25 @@
     return pltpu.with_memory_space_constraint(x, pltpu.HBM)
 
 
-def pick(sub_count, block, own_map, rows, tail):
+def pick_lead(sub_count, block, own_map, rows, lead):
+    width = 2 * block
+    return pl.pallas_call(
+        functools.partial(lead_kernel, sub_count, block),
+        in_specs=[HB, HB],
+        out_specs=VM,
+        out_shape=pltpu.VMEM((lead, width), rows.dtype),
+        scratch_shapes=[
+            pltpu.SMEM(own_map.shape, jnp.int32),
+            pltpu.VMEM((lead, rows.shape[1]), rows.dtype),
+            pltpu.SemaphoreType.DMA((2,)),
+        ],
+        compiler_params=pltpu.CompilerParams(vmem_limit_bytes=2 << 20),
+        cost_estimate=cost(lead * block, 8 * lead * block),
+        name="lead",
+    )(own_map, rows)
+
+
+def pick(sub_count, block, own_map, rows, lead, tail):
     depth = rows.shape[0]
     width = 2 * block
     return pl.pallas_call(
@@ -476,7 +519,7 @@
         in_specs=[HB, HB],
         out_specs=[VM] * 3,
         out_shape=[
-            pltpu.VMEM((depth, width), rows.dtype),
+            pltpu.VMEM((depth - lead, width), rows.dtype),
             pltpu.VMEM((depth - tail, width), rows.dtype),
             pltpu.VMEM((tail, width), rows.dtype),
         ],
@@ -488,7 +531,7 @@
         compiler_params=pltpu.CompilerParams(vmem_limit_bytes=4 << 20),
         cost_estimate=cost(depth * block, 8 * depth * block),
         name="pick",
-    )(in_hbm(own_map), in_hbm(rows))
+    )(own_map, rows)
 
 
 def pair_shards(
@@ -516,8 +559,11 @@
         (2 * i + c, 2 * ((i - 1) % sub_count) + 1 - c) for i in range(sub_count) for c in range(2)
     ]
     params = pltpu.CompilerParams(vmem_limit_bytes=12 << 20)
-    mine, head, tail = pick(sub_count, block, block_map, interface_coupling[0], depth // 4)
-    got_theirs = in_vmem(lax.ppermute(mine, "col", swap))
+    own_map, coupling_rows = in_hbm(block_map), in_hbm(interface_coupling[0])
+    lead = pick_lead(sub_count, block, own_map, coupling_rows, depth // 4)
+    got_lead = in_vmem(lax.ppermute(lead, "col", swap))
+    rest, head, tail = pick(sub_count, block, own_map, coupling_rows, depth // 4, depth // 12)
+    got_rest = in_vmem(lax.ppermute(rest, "col", swap))
     got_head = in_vmem(lax.ppermute(head, "col", swap))
     got_tail = in_vmem(lax.ppermute(tail, "col", swap))
     previous_trial = shifted(trial_vectors, "sub", 1)
@@ -530,7 +576,7 @@
 
     turned, before_mine, before_theirs, columns = pl.pallas_call(
         functools.partial(local_kernel, tile),
-        in_specs=[VM] * 5,
+        in_specs=[VM] * 6,
         out_specs=[VM] * 4,
         out_shape=[
             pltpu.VMEM((2 * width, depth), BF16),
@@ -541,10 +587,10 @@
         compiler_params=params,
         cost_estimate=cost(4 * depth * depth * width, 2 * depth * depth),
         name="local",
-    )(inverse_rows, mine, head, tail, in_vmem(interior_mass))
+    )(inverse_rows, lead, rest, head, tail, in_vmem(interior_mass))
     stiff_low, stiff_high, square, turned_w, small_first = pl.pallas_call(
         functools.partial(first_kernel, tile, sub_count, block),
-        in_specs=[SM] + [VM] * 10,
+        in_specs=[SM] + [VM] * 11,
         out_specs=[VM] * 5,
         out_shape=[
             pltpu.VMEM((width, width), BF16),
@@ -560,7 +606,8 @@
     )(
         block_map,
         inverse_rows,
-        got_theirs,
+        got_lead,
+        got_rest,
         before_theirs,
         columns,
         turned,

time: 61 us -> 64 us (1.049)
  Pallas kernels: 13.6 us -> 15.1 us
  waiting for transfers between devices: 29.5 us -> 31 us
    ppermute x1 -> x2, waiting for transfers between devices: 0.01 us -> 23.6 us  [the longest x1 23.6 us: pair_shards(): got_lead = in_vmem(lax.ppermute(lead, 'col', swap))]
    ppermute x1, waiting for transfers between devices: 22.5 us -> 0.01 us  [pair_shards(): got_head = in_vmem(lax.ppermute(head, 'col', swap))]
    ppermute x1 -> x2, starting transfers between devices: 3.03 us -> 5.04 us  [the longest x1 3.03 us: pair_shards(): got_rest = in_vmem(lax.ppermute(rest, 'col', swap))]
    ppermute x1, starting transfers between devices: 1.95 us -> 0.15 us  [pair_shards(): got_tail = in_vmem(lax.ppermute(tail, 'col', swap))]
    pallas_call x1 -> x2, Pallas kernels: 2.81 us -> 4.11 us  [the longest x1 3.06 us: pair_shards(): pl.pallas_call(functools.partial(local_kernel, tile), in_specs=[VM] * 6,...]
  transfers between devices with their start and end apart: 9 -> 10, of which waited for: 4 -> 4; matrix products, arithmetic and copies ran while one was open for 0% -> 0% of each run, Pallas kernels for 13% -> 16%
where the time goes in v3:
time: 64 us; the launch traced here: 63.8 us
  waiting for transfers between devices  31 us (48%)
  Pallas kernels  15.1 us (24%)
  starting transfers between devices  13.1 us (20%)
  local copies, waits for them, and re-layouts  3.72 us (6%)
  between operations  0.79 us (1%)
    ppermute x1, waiting for transfers between devices, pair_shards(): got_lead = in_vmem(lax.ppermute(lead, 'col', swap))  23.6 us
    ppermute x1, waiting for transfers between devices, pair_shards(): cross_mass = lax.ppermute(mass_low, both, cross_route)  4.99 us
    unnamed x18, local copies, waits for them, and re-layouts  3.72 us
    pallas_call x1, Pallas kernels, pair_shards(): pl.pallas_call(functools.partial(first_kernel, tile, sub_count, block), i...  3.24 us
    pallas_call x1, Pallas kernels, pair_shards(): pl.pallas_call(functools.partial(local_kernel, tile), in_specs=[VM] * 6,...  3.06 us
    ppermute x1, starting transfers between devices, pair_shards(): got_rest = in_vmem(lax.ppermute(rest, 'col', swap))  3.03 us
    ppermute x1, starting transfers between devices, pair_shards(): back_here = lax.ppermute(back, 'sub', back_route)  2.74 us
    pallas_call x2, Pallas kernels, place(): pl.pallas_call(functools.partial(place_kernel, which, sub_count, block),...  2.33 us
  transfers between devices with their start and end apart: 10, of which 4 were waited for; matrix products, arithmetic and copies ran while one was open for 0% of the time, Pallas kernels for 16%

profile of v3, /device:TPU:0, one launch (start us, length us, event | category | flops | bytes accessed | tf_op | source)
XLA Modules:
  0.0 63.8 jit_solution(9305173590363917693)
XLA Ops:
  0.7 1.6 %pick.1 = (bf16[1152,256]{1,0:T(8,128)(2,1)S(1)}, bf16[1408,256]{1,0:T(8,128)(2,1)S(1)}, bf16[128,256]{1,0:T(8,128)(2,1)S(1)}) custom-call(s32[1,4]{1,0:T(1,128)} %map_ref.7, bf16[1536,512]{1,0:T(8,128)(2,1)} %bitcast.28), custom_call_target="tpu_custom_call" | custom-call | flops 196608 | bytes 1572864 | tf_op jit(solution)/shard_map/pick/pallas_call | solution.py:517
  2.3 3.0 %collective-permute-start.3 = (bf16[1152,256]{1,0:T(8,128)(2,1)S(1)}, bf16[1152,256]{1,0:T(8,128)(2,1)S(1)}, u32[]{:S(2)}, u32[]{:S(2)}) collective-permute-start(bf16[1152,256]{1,0:T(8,128)(2,1)S(1)} %get-tuple-element.28.rest_ref), channel_id=1, source_target_pairs={{0,1},{1,0},{2,3},{3,2},{4,5},{5,4},{6,7},{7,6},{8,9},{9,8},{10,11... | collective-permute-start | bytes 1769480 | tf_op jit(solution)/shard_map/ppermute | solution.py:566
  5.3 0.1 collective-permute-start.1
  5.4 1.0 %lead.1.lead_ref = bf16[384,256]{1,0:T(8,128)(2,1)S(1)} custom-call(s32[1,4]{1,0:T(1,128)} %map_ref.7, bf16[1536,512]{1,0:T(8,128)(2,1)} %bitcast.29), custom_call_target="tpu_custom_call" | custom-call | flops 49152 | bytes 393216 | tf_op jit(solution)/shard_map/lead/pallas_call | solution.py:498
  6.5 2.0 %collective-permute-start.2 = (bf16[384,256]{1,0:T(8,128)(2,1)S(1)}, bf16[384,256]{1,0:T(8,128)(2,1)S(1)}, u32[]{:S(2)}, u32[]{:S(2)}) collective-permute-start(bf16[384,256]{1,0:T(8,128)(2,1)S(1)} %lead.1.lead_ref), channel_id=1, source_target_pairs={{0,1},{1,0},{2,3},{3,2},{4,5},{5,4},{6,7},{7,6},{8,9},{9,8},{10,11... | collective-permute-start | bytes 589832 | tf_op jit(solution)/shard_map/ppermute | solution.py:564
  8.5 0.0 copy-done.7
  8.5 0.0 collective-permute-start.4
  8.5 0.1 collective-permute-start
  8.6 3.7 %copy-done = bf16[1,1536,3072]{2,1,0:T(8,128)(2,1)S(1)} copy-done((bf16[1,1536,3072]{2,1,0:T(8,128)(2,1)S(1)}, bf16[1,1536,3072]{2,1,0:T(8,128)(2,1)}, u32[]{:S(2)}) %copy-start) | copy-done | bytes 9437208
  12.3 0.0 copy-start.6
  12.3 3.1 %local.1 = (bf16[512,1536]{1,0:T(8,128)(2,1)S(1)}, f32[1536,256]{1,0:T(8,128)S(1)}, f32[1536,256]{1,0:T(8,128)S(1)}, f32[1536,128]{1,0:T(8,128)S(1)}) custom-call(bf16[1536,3072]{1,0:T(8,128)(2,1)S(1)} %bitcast.14, bf16[384,256]{1,0:T(8,128)(2,1)S(1)} %lead.1.lead_ref, bf16[1152,256]{1,0:T(8,128)(2,1)S(1)} %get-tuple-element.28.rest_ref, ...), custom_call_target="tpu_custom_call" | custom-call | flops 2415919104 | bytes 4718592 | tf_op jit(solution)/shard_map/local/pallas_call | solution.py:577
  15.4 0.0 collective-permute-done.4
  15.5 23.6 %collective-permute-done.2.lead_ref = bf16[384,256]{1,0:T(8,128)(2,1)S(1)} collective-permute-done((bf16[384,256]{1,0:T(8,128)(2,1)S(1)}, bf16[384,256]{1,0:T(8,128)(2,1)S(1)}, u32[]{:S(2)}, u32[]{:S(2)}) %collective-permute-start.2) | collective-permute-done | bytes 196640 | tf_op jit(solution)/shard_map/ppermute | solution.py:564
  39.0 0.0 collective-permute-done.3.rest_ref
  39.1 3.2 %first.1 = (bf16[256,256]{1,0:T(8,128)(2,1)S(1)}, bf16[256,256]{1,0:T(8,128)(2,1)S(1)}, bf16[256,256]{1,0:T(8,128)(2,1)S(1)}, bf16[256,1536]{1,0:T(8,128)(2,1)S(1)}, f32[64,200]{1,0:T(8,128)S(1)}) custom-call(s32[1,4]{1,0:T(1,128)S(1)} %copy-done.4, bf16[1536,3072]{1,0:T(8,128)(2,1)S(1)} %bitcast.15, bf16[384,256]{1,0:T(8,128)(2,1)S(1)} %collective-permute-done.2.lead_ref, ...), custom_call_target="tpu_custom_call" | custom-call | flops 2415919104 | bytes 4718592 | tf_op jit(solution)/shard_map/first/pallas_call | solution.py:591
  42.3 0.0 collective-permute-done.1.got_ref
  42.3 1.4 %middle.1.before_ref = f32[1536,256]{1,0:T(8,128)S(1)} custom-call(bf16[1536,3072]{1,0:T(8,128)(2,1)S(1)} %bitcast.16, bf16[1408,256]{1,0:T(8,128)(2,1)S(1)} %collective-permute-done.1.got_ref, f32[1536,256]{1,0:T(8,128)S(1)} %get-tuple-element.29.before_ref), custom_call_target="tpu_custom_call" | custom-call | flops 1207959552 | bytes 4718592 | tf_op jit(solution)/shard_map/middle/pallas_call | solution.py:622
  43.7 0.0 collective-permute-done.got_ref
  43.7 1.1 %second.1 = (bf16[256,256]{1,0:T(8,128)(2,1)S(1)}, bf16[320,256]{1,0:T(8,128)(2,1)S(1)}, bf16[1536,256]{1,0:T(8,128)(2,1)S(1)}, bf16[1536,256]{1,0:T(8,128)(2,1)...) custom-call(bf16[1536,3072]{1,0:T(8,128)(2,1)S(1)} %bitcast.17, bf16[128,256]{1,0:T(8,128)(2,1)S(1)} %collective-permute-done.got_ref, ...), custom_call_target="tpu_custom_call" | custom-call | flops 1207959552 | bytes 4718592 | tf_op jit(solution)/shard_map/second/pallas_call | solution.py:631
  44.8 1.4 %third.1 = (bf16[2,256,256]{2,1,0:T(8,128)(2,1)S(1)}, f32[2,256,256]{2,1,0:T(8,128)S(1)}) custom-call(s32[1,4]{1,0:T(1,128)S(1)} %copy-done.4, bf16[1536,256]{1,0:T(8,128)(2,1)S(1)} %get-tuple-element.36.g_ref, bf16[1536,256]{1,0:T(8,128)(2,1)S(1)} %get-tuple-element.37.w_ref, f32[256,256]{1,0:T(8,128)S(1)} %get-tuple-element.38.crossed_ref, ...), custom_call_target="tpu_custom_call" | custom-call | flops 805306368 | bytes 3932160 | tf_op jit(solution)/shard_map/third/pallas_call | solution.py:658
  46.2 2.7 %collective-permute-start.6 = (bf16[2,256,256]{2,1,0:T(8,128)(2,1)S(1)}, bf16[2,256,256]{2,1,0:T(8,128)(2,1)S(1)}, u32[]{:S(2)}, u32[]{:S(2)}) collective-permute-start(bf16[2,256,256]{2,1,0:T(8,128)(2,1)S(1)} %get-tuple-element.41), channel_id=1, source_target_pairs={{0,30},{2,0},{4,2},{6,4},{8,6},{10,8},{12,10},{14,12},{16,14},{18,... | collective-permute-start | bytes 786440 | tf_op jit(solution)/shard_map/ppermute | solution.py:667
  48.9 1.5 %collective-permute-start.8 = (bf16[320,256]{1,0:T(8,128)(2,1)S(1)}, bf16[320,256]{1,0:T(8,128)(2,1)S(1)}, u32[]{:S(2)}, u32[]{:S(2)}) collective-permute-start(bf16[320,256]{1,0:T(8,128)(2,1)S(1)} %get-tuple-element.45), channel_id=1, source_target_pairs={{0,1},{1,0},{2,3},{3,2},{4,5},{5,4},{6,7},{7,6},{8,9},{9,8},{10,11... | collective-permute-start | bytes 491528 | tf_op jit(solution)/shard_map/ppermute | solution.py:669
  50.4 1.9 %collective-permute-start.9 = (bf16[256,256]{1,0:T(8,128)(2,1)S(1)}, bf16[256,256]{1,0:T(8,128)(2,1)S(1)}, u32[]{:S(2)}, u32[]{:S(2)}) collective-permute-start(bf16[256,256]{1,0:T(8,128)(2,1)S(1)} %get-tuple-element.46), channel_id=1, source_target_pairs={{0,31},{1,30},{2,1},{3,0},{4,3},{5,2},{6,5},{7,4},{8,7},{9,6},{10,... | collective-permute-start | bytes 393224 | tf_op jit(solution)/shard_map/ppermute | solution.py:668
  52.3 1.5 %collective-permute-start.5 = (bf16[256,256]{1,0:T(8,128)(2,1)S(1)}, bf16[256,256]{1,0:T(8,128)(2,1)S(1)}, u32[]{:S(2)}, u32[]{:S(2)}) collective-permute-start(bf16[256,256]{1,0:T(8,128)(2,1)S(1)} %get-tuple-element.40), channel_id=1, source_target_pairs={{0,1},{1,0},{2,3},{3,2},{4,5},{5,4},{6,7},{7,6},{8,9},{9,8},{10,11... | collective-permute-start | bytes 393224 | tf_op jit(solution)/shard_map/ppermute | solution.py:621
  53.9 0.2 collective-permute-start.7
  54.0 5.0 %collective-permute-done.9.cross_ref = bf16[256,256]{1,0:T(8,128)(2,1)S(1)} collective-permute-done((bf16[256,256]{1,0:T(8,128)(2,1)S(1)}, bf16[256,256]{1,0:T(8,128)(2,1)S(1)}, u32[]{:S(2)}, u32[]{:S(2)}) %collective-permute-start.9) | collective-permute-done | bytes 131104 | tf_op jit(solution)/shard_map/ppermute | solution.py:668
  59.0 0.0 collective-permute-done.8.high_ref
  59.0 0.0 collective-permute-done.6.back_ref
  59.0 1.2 %shard_map.104 = (bf16[2,128,16,128]{3,2,1,0:T(8,128)(2,1)}, f32[64,200]{1,0:T(8,128)}) custom-call(f32[2,256,256]{2,1,0:T(8,128)S(1)} %get-tuple-element.39.own_ref, bf16[320,256]{1,0:T(8,128)(2,1)S(1)} %collective-permute-done.8.high_ref, bf16[2,256,256]{2,1,0:T(8,128)(2,1)S(1)} %collective-permute-done.6.back_ref, ...), custom_call_target="tpu_custom_call" | custom-call | flops 4194304 | bytes 1048576 | tf_op jit(solution)/shard_map/pallas_call | solution.py:472
  60.2 0.4 collective-permute-done.5.high_ref
  60.6 2.0 %collective-permute-done.7.cross_ref = bf16[256,256]{1,0:T(8,128)(2,1)S(1)} collective-permute-done((bf16[256,256]{1,0:T(8,128)(2,1)S(1)}, bf16[256,256]{1,0:T(8,128)(2,1)S(1)}, u32[]{:S(2)}, u32[]{:S(2)}) %collective-permute-start.7) | collective-permute-done | bytes 131104 | tf_op jit(solution)/shard_map/ppermute | solution.py:620
  62.7 1.2 %shard_map.103 = (bf16[2,128,16,128]{3,2,1,0:T(8,128)(2,1)}, f32[8,128]{1,0:T(8,128)}) custom-call(f32[2,256,256]{2,1,0:T(8,128)S(1)} %get-tuple-element.39.own_ref, bf16[256,256]{1,0:T(8,128)(2,1)S(1)} %collective-permute-done.5.high_ref, bf16[2,256,256]{2,1,0:T(8,128)(2,1)S(1)} %collective-permute-done.6.back_ref, ...), custom_call_target="tpu_custom_call" | custom-call | flops 4194304 | bytes 1048576 | tf_op jit(solution)/shard_map/pallas_call | solution.py:472
  (15 shorter events, 0.0 us)
Async XLA Ops:
  0.6 7.9 %copy-start.7 = (bf16[64,2,128]{2,1,0:T(2,128)(2,1)S(1)}, bf16[64,2,128]{2,1,0:T(2,128)(2,1)}, u32[]{:S(2)}) copy-start(bf16[64,2,128]{2,1,0:T(2,128)(2,1)} %param.15) | copy-start | bytes 98308
  0.6 8.0 %copy-start.5 = (f32[1,1536]{1,0:T(1,128)S(1)}, f32[1,1536]{1,0:T(1,128)}, u32[]{:S(2)}) copy-start(f32[1,1536]{1,0:T(1,128)} %mass_ref.1) | copy-start | bytes 18436
  2.3 36.7 %collective-permute-start.3 = (bf16[1152,256]{1,0:T(8,128)(2,1)S(1)}, bf16[1152,256]{1,0:T(8,128)(2,1)S(1)}, u32[]{:S(2)}, u32[]{:S(2)}) collective-permute-start(bf16[1152,256]{1,0:T(8,128)(2,1)S(1)} %get-tuple-element.28.rest_ref), channel_id=1, source_target_pairs={{0,1},{1,0},{2,3},{3,2},{4,5},{5,4},{6,7},{7,6},{8,9},{9,8},{10,11... | collective-permute-start | bytes 1769480 | tf_op jit(solution)/shard_map/ppermute | solution.py:566
  5.3 37.0 %collective-permute-start.1 = (bf16[1408,256]{1,0:T(8,128)(2,1)S(1)}, bf16[1408,256]{1,0:T(8,128)(2,1)S(1)}, u32[]{:S(2)}, u32[]{:S(2)}) collective-permute-start(bf16[1408,256]{1,0:T(8,128)(2,1)S(1)} %get-tuple-element.27.head_ref), channel_id=1, source_target_pairs={{0,1},{1,0},{2,3},{3,2},{4,5},{5,4},{6,7},{7,6},{8,9},{9,8},{10,11... | collective-permute-start | bytes 2162696 | tf_op jit(solution)/shard_map/ppermute | solution.py:567
  6.5 32.6 %collective-permute-start.2 = (bf16[384,256]{1,0:T(8,128)(2,1)S(1)}, bf16[384,256]{1,0:T(8,128)(2,1)S(1)}, u32[]{:S(2)}, u32[]{:S(2)}) collective-permute-start(bf16[384,256]{1,0:T(8,128)(2,1)S(1)} %lead.1.lead_ref), channel_id=1, source_target_pairs={{0,1},{1,0},{2,3},{3,2},{4,5},{5,4},{6,7},{7,6},{8,9},{9,8},{10,11... | collective-permute-start | bytes 589832 | tf_op jit(solution)/shard_map/ppermute | solution.py:564
  8.5 6.9 %collective-permute-start.4 = (bf16[64,2,128]{2,1,0:T(2,128)(2,1)S(1)}, bf16[64,2,128]{2,1,0:T(2,128)(2,1)S(1)}, u32[]{:S(2)}, u32[]{:S(2)}) collective-permute-start(bf16[64,2,128]{2,1,0:T(2,128)(2,1)S(1)} %copy-done.7), channel_id=1, source_target_pairs={{30,0},{0,2},{2,4},{4,6},{6,8},{8,10},{10,12},{12,14},{14,16},{16,... | collective-permute-start | bytes 98312 | tf_op jit(solution)/shard_map/ppermute | solution.py:13
  8.5 35.2 %collective-permute-start = (bf16[128,256]{1,0:T(8,128)(2,1)S(1)}, bf16[128,256]{1,0:T(8,128)(2,1)S(1)}, u32[]{:S(2)}, u32[]{:S(2)}) collective-permute-start(bf16[128,256]{1,0:T(8,128)(2,1)S(1)} %get-tuple-element.26.tail_ref), channel_id=1, source_target_pairs={{0,1},{1,0},{2,3},{3,2},{4,5},{5,4},{6,7},{7,6},{8,9},{9,8},{10,11... | collective-permute-start | bytes 196616 | tf_op jit(solution)/shard_map/ppermute | solution.py:568
  8.6 3.7 %copy-start = (bf16[1,1536,3072]{2,1,0:T(8,128)(2,1)S(1)}, bf16[1,1536,3072]{2,1,0:T(8,128)(2,1)}, u32[]{:S(2)}) copy-start(bf16[1,1536,3072]{2,1,0:T(8,128)(2,1)} %param.8) | copy-start | bytes 28311556
  12.3 26.7 %copy-start.1 = (bf16[1,1536,3072]{2,1,0:T(8,128)(2,1)S(1)}, bf16[1,1536,3072]{2,1,0:T(8,128)(2,1)}, u32[]{:S(2)}) copy-start(bf16[1,1536,3072]{2,1,0:T(8,128)(2,1)} %param.8) | copy-start | bytes 28311556
  12.3 26.7 %copy-start.2 = (bf16[1,200,1536]{2,1,0:T(8,128)(2,1)S(1)}, bf16[1,200,1536]{2,1,0:T(8,128)(2,1)}, u32[]{:S(2)}) copy-start(bf16[1,200,1536]{2,1,0:T(8,128)(2,1)} %param.13) | copy-start | bytes 1843204
  12.3 26.7 %copy-start.3 = (f32[1,256,512]{2,1,0:T(8,128)S(1)}, f32[1,256,512]{2,1,0:T(8,128)}, u32[]{:S(2)}) copy-start(f32[1,256,512]{2,1,0:T(8,128)} %param.10) | copy-start | bytes 1572868
  12.3 26.7 %copy-start.4 = (s32[1,4]{1,0:T(1,128)S(1)}, s32[1,4]{1,0:T(1,128)}, u32[]{:S(2)}) copy-start(s32[1,4]{1,0:T(1,128)} %map_ref.7) | copy-start | bytes 52
  12.3 26.7 %copy-start.6 = (f32[1,256]{1,0:T(1,128)S(1)}, f32[1,256]{1,0:T(1,128)}, u32[]{:S(2)}) copy-start(f32[1,256]{1,0:T(1,128)} %param.12) | copy-start | bytes 3076
  46.2 12.9 %collective-permute-start.6 = (bf16[2,256,256]{2,1,0:T(8,128)(2,1)S(1)}, bf16[2,256,256]{2,1,0:T(8,128)(2,1)S(1)}, u32[]{:S(2)}, u32[]{:S(2)}) collective-permute-start(bf16[2,256,256]{2,1,0:T(8,128)(2,1)S(1)} %get-tuple-element.41), channel_id=1, source_target_pairs={{0,30},{2,0},{4,2},{6,4},{8,6},{10,8},{12,10},{14,12},{16,14},{18,... | collective-permute-start | bytes 786440 | tf_op jit(solution)/shard_map/ppermute | solution.py:667
  48.9 10.1 %collective-permute-start.8 = (bf16[320,256]{1,0:T(8,128)(2,1)S(1)}, bf16[320,256]{1,0:T(8,128)(2,1)S(1)}, u32[]{:S(2)}, u32[]{:S(2)}) collective-permute-start(bf16[320,256]{1,0:T(8,128)(2,1)S(1)} %get-tuple-element.45), channel_id=1, source_target_pairs={{0,1},{1,0},{2,3},{3,2},{4,5},{5,4},{6,7},{7,6},{8,9},{9,8},{10,11... | collective-permute-start | bytes 491528 | tf_op jit(solution)/shard_map/ppermute | solution.py:669
  50.4 8.6 %collective-permute-start.9 = (bf16[256,256]{1,0:T(8,128)(2,1)S(1)}, bf16[256,256]{1,0:T(8,128)(2,1)S(1)}, u32[]{:S(2)}, u32[]{:S(2)}) collective-permute-start(bf16[256,256]{1,0:T(8,128)(2,1)S(1)} %get-tuple-element.46), channel_id=1, source_target_pairs={{0,31},{1,30},{2,1},{3,0},{4,3},{5,2},{6,5},{7,4},{8,7},{9,6},{10,... | collective-permute-start | bytes 393224 | tf_op jit(solution)/shard_map/ppermute | solution.py:668
  52.3 8.3 %collective-permute-start.5 = (bf16[256,256]{1,0:T(8,128)(2,1)S(1)}, bf16[256,256]{1,0:T(8,128)(2,1)S(1)}, u32[]{:S(2)}, u32[]{:S(2)}) collective-permute-start(bf16[256,256]{1,0:T(8,128)(2,1)S(1)} %get-tuple-element.40), channel_id=1, source_target_pairs={{0,1},{1,0},{2,3},{3,2},{4,5},{5,4},{6,7},{7,6},{8,9},{9,8},{10,11... | collective-permute-start | bytes 393224 | tf_op jit(solution)/shard_map/ppermute | solution.py:621
  53.9 8.8 %collective-permute-start.7 = (bf16[256,256]{1,0:T(8,128)(2,1)S(1)}, bf16[256,256]{1,0:T(8,128)(2,1)S(1)}, u32[]{:S(2)}, u32[]{:S(2)}) collective-permute-start(bf16[256,256]{1,0:T(8,128)(2,1)S(1)} %get-tuple-element.42), channel_id=1, source_target_pairs={{0,31},{1,30},{2,1},{3,0},{4,3},{5,2},{6,5},{7,4},{8,7},{9,6},{10,... | collective-permute-start | bytes 393224 | tf_op jit(solution)/shard_map/ppermute | solution.py:620
